TPU v7x, 32 devices: a whole 2x2x4 slice. The times are simulated.
32 devices in a mesh: dp: 8 (over z, x), mp: 4 (over y, core).
Axes of the slice: x: 2, y: 2, z: 4, core: 2. Of those that a mesh axis runs over, the one named last changes fastest.
Arguments:
- token_ids: int32 [8, 1024], P('dp'), may hold values from 0 to 50303
- target_ids: int32 [8, 1024], P('dp'), may hold values from 0 to 50303
- segment_ids: int32 [8, 1024], P('dp'), may hold values from 0 to 3, never falling along the last dimension, each value on 1 to 512 neighbouring positions
- domain_ids: int32 [8, 1024], P('dp'), may hold values from 0 to 7, as said below
- domain_weights: int32 [8], replicated, may hold values from 1 to 8
- table: float32 [50304, 1024], P(('dp', 'mp')), may hold values from -0.375 to 0.375
- attn_weights: float32 [4, 1024, 1024], P(None, 'dp', 'mp'), may hold values from -0.1875 to 0.1875
- out_weights: float32 [1024, 1024], P('mp', 'dp'), may hold values from -0.1875 to 0.1875
- ffn_weights: float32 [2, 1024, 2816], P(None, 'dp', 'mp'), may hold values from -0.1875 to 0.1875
- down_weights: float32 [2816, 1024], P('mp', 'dp'), may hold values from -0.02734375 to 0.02734375
- gains: float32 [4, 1024], P(None, 'dp'), may hold values from 0.5 to 1.5
- table_moment: float32 [50304, 1024], P(('dp', 'mp')), may hold values from -0.00018310547 to 0.00018310547
- attn_moment: float32 [4, 1024, 1024], P(None, 'dp', 'mp'), may hold values from -0.00018310547 to 0.00018310547
- out_moment: float32 [1024, 1024], P('mp', 'dp'), may hold values from -0.00018310547 to 0.00018310547
- ffn_moment: float32 [2, 1024, 2816], P(None, 'dp', 'mp'), may hold values from -0.00018310547 to 0.00018310547
- down_moment: float32 [2816, 1024], P('mp', 'dp'), may hold values from -0.00018310547 to 0.00018310547
- gain_moment: float32 [4, 1024], P(None, 'dp'), may hold values from -0.0009765625 to 0.0009765625
- table_average: float32 [50304, 1024], P(('dp', 'mp')), may hold values from -0.375 to 0.375
- attn_average: float32 [4, 1024, 1024], P(None, 'dp', 'mp'), may hold values from -0.1875 to 0.1875
- out_average: float32 [1024, 1024], P('mp', 'dp'), may hold values from -0.1875 to 0.1875
- ffn_average: float32 [2, 1024, 2816], P(None, 'dp', 'mp'), may hold values from -0.1875 to 0.1875
- down_average: float32 [2816, 1024], P('mp', 'dp'), may hold values from -0.02734375 to 0.02734375
- gain_average: float32 [4, 1024], P(None, 'dp'), may hold values from 0.5 to 1.5
Outputs:
- total_loss: float32 [], replicated
- domain_loss: float32 [8], replicated
- grad_norm: float32 [], replicated
- new_table_moment: float32 [50304, 1024], P(('dp', 'mp'))
- new_table: float32 [50304, 1024], P(('dp', 'mp'))
- new_table_average: float32 [50304, 1024], P(('dp', 'mp'))
- new_attn_moment: float32 [4, 1024, 1024], P(None, 'dp', 'mp')
- new_attn: float32 [4, 1024, 1024], P(None, 'dp', 'mp')
- new_attn_average: float32 [4, 1024, 1024], P(None, 'dp', 'mp')
- new_out_moment: float32 [1024, 1024], P('mp', 'dp')
- new_out: float32 [1024, 1024], P('mp', 'dp')
- new_out_average: float32 [1024, 1024], P('mp', 'dp')
- new_ffn_moment: float32 [2, 1024, 2816], P(None, 'dp', 'mp')
- new_ffn: float32 [2, 1024, 2816], P(None, 'dp', 'mp')
- new_ffn_average: float32 [2, 1024, 2816], P(None, 'dp', 'mp')
- new_down_moment: float32 [2816, 1024], P('mp', 'dp')
- new_down: float32 [2816, 1024], P('mp', 'dp')
- new_down_average: float32 [2816, 1024], P('mp', 'dp')
- new_gain_moment: float32 [4, 1024], P(None, 'dp')
- new_gains: float32 [4, 1024], P(None, 'dp')
- new_gain_average: float32 [4, 1024], P(None, 'dp')
Inputs may be any that keep to these rules, and one draw needn't show every extreme that they name: `segment_ids`: segment ids never fall along a sequence; each sequence holds 4 documents. `domain_ids`: A domain may hold no token at all.
All inputs are finite; a program needn't handle non-finite values.
Results may differ from a plain program's by a relative error of at most 0.0083.
Values may be sent and summed in bfloat16 or wider, within the bound.
A program may use at most 320 MiB of HBM per device.

v0:
```python
import jax
import jax.numpy as jnp
from jax import lax
from jax.sharding import PartitionSpec as P

HD = 64
DOMAINS = 8


EPSILON = 1e-06
CLIP_NORM = 0.01
LEARN_RATE = 1000.0
MOMENTUM = 0.9
AVERAGE_KEEP = 0.75
MASKED = -1e30


def normed(values, gain):
    factor = lax.rsqrt(jnp.mean(values * values, axis=-1, keepdims=True) + EPSILON)
    return (values * factor * gain, factor)


def normed_back(values, factor, gain, upward):
    gained = gain * upward
    inward = factor * gained - values * (factor * factor * factor) * jnp.mean(
        gained * values, axis=-1, keepdims=True
    )
    return (inward, jnp.sum(upward * values * factor, axis=0))


def rotary_tables(length, half):
    places = jnp.arange(length, dtype=jnp.float32)[:, None]
    speeds = 10000.0 ** (-jnp.arange(half, dtype=jnp.float32) / half)
    angles = places * speeds
    return (jnp.cos(angles)[:, None, :], jnp.sin(angles)[:, None, :])


def rotate(values, cosine, sine, direction):
    half = values.shape[-1] // 2
    first = values[..., :half]
    second = values[..., half:]
    return jnp.concatenate(
        [first * cosine - direction * second * sine, second * cosine + direction * first * sine],
        axis=-1,
    )


def block_scores(queries, keys, segments, offset, block_rows):
    query_block = lax.dynamic_slice_in_dim(queries, offset, block_rows, 0)
    query_segments = lax.dynamic_slice_in_dim(segments, offset, block_rows, 0)
    places = jnp.arange(segments.shape[0], dtype=jnp.int32)
    query_places = offset + jnp.arange(block_rows, dtype=jnp.int32)
    allowed = (query_places[:, None] >= places[None, :]) & (
        query_segments[:, None] == segments[None, :]
    )
    raw_scores = jnp.einsum(
        "qhd,khd->hqk", query_block, keys, preferred_element_type=jnp.float32
    ) * HD ** (-0.5)
    return (jnp.where(allowed[None], raw_scores, MASKED), query_block)


def attend_forward(queries, keys, values, segments, block_rows):
    length = queries.shape[0]

    def one_block(offset):
        scores, query_block = block_scores(queries, keys, segments, offset, block_rows)
        highest = jnp.max(scores, axis=-1, keepdims=True)
        raised = jnp.exp(scores - highest)
        totals = jnp.sum(raised, axis=-1, keepdims=True)
        mixed = jnp.einsum(
            "hqk,khd->qhd",
            (raised / totals).astype(jnp.bfloat16),
            values,
            preferred_element_type=jnp.float32,
        )
        return (mixed, (highest + jnp.log(totals))[..., 0])

    offsets = jnp.arange(length // block_rows, dtype=jnp.int32) * block_rows
    mixed, log_totals = lax.map(one_block, offsets)
    return (mixed.reshape(length, queries.shape[1], queries.shape[2]), log_totals)


def attend_backward(queries, keys, values, segments, log_totals, out_grad, block_rows):
    length = queries.shape[0]

    def one_block(carry, inputs):
        offset, block_totals = inputs
        key_grad, value_grad = carry
        scores, query_block = block_scores(queries, keys, segments, offset, block_rows)
        grad_block = lax.dynamic_slice_in_dim(out_grad, offset, block_rows, 0)
        soft_probs = jnp.exp(scores - block_totals[..., None])
        prob_grad = jnp.einsum(
            "qhd,khd->hqk", grad_block, values, preferred_element_type=jnp.float32
        )
        inner = jnp.sum(prob_grad * soft_probs, axis=-1, keepdims=True)
        score_grad = (soft_probs * (prob_grad - inner)).astype(jnp.bfloat16)
        query_grad = jnp.einsum(
            "hqk,khd->qhd", score_grad, keys, preferred_element_type=jnp.float32
        ) * HD ** (-0.5)
        key_grad = key_grad + jnp.einsum(
            "hqk,qhd->khd", score_grad, query_block, preferred_element_type=jnp.float32
        ) * HD ** (-0.5)
        value_grad = value_grad + jnp.einsum(
            "hqk,qhd->khd",
            soft_probs.astype(jnp.bfloat16),
            grad_block,
            preferred_element_type=jnp.float32,
        )
        return ((key_grad, value_grad), query_grad)

    empty = jnp.zeros(keys.shape, jnp.float32)
    offsets = jnp.arange(length // block_rows, dtype=jnp.int32) * block_rows
    (key_grad, value_grad), query_grad = lax.scan(one_block, (empty, empty), (offsets, log_totals))
    return (query_grad.reshape(queries.shape), key_grad, value_grad)


def contract_rows(left, right):
    return lax.dot_general(
        left, right, (((0,), (0,)), ((), ())), preferred_element_type=jnp.float32
    )


def contract_last(left, right):
    return lax.dot_general(
        left, right, (((1,), (1,)), ((), ())), preferred_element_type=jnp.float32
    )


def owned_rows(ids, shard_rows, groups, member):
    blocks = ids // shard_rows
    inside = blocks % groups == member
    local_ids = blocks // groups * shard_rows + ids % shard_rows
    return (inside, local_ids)


def per_device(
    token_ids,
    target_ids,
    segment_ids,
    domain_ids,
    domain_weights,
    table,
    attn_weights,
    out_weights,
    ffn_weights,
    down_weights,
    gains,
    table_moment,
    attn_moment,
    out_moment,
    ffn_moment,
    down_moment,
    gain_moment,
    table_average,
    attn_average,
    out_average,
    ffn_average,
    down_average,
    gain_average,
):
    masters = (table, attn_weights, out_weights, ffn_weights, down_weights, gains)
    moments = (table_moment, attn_moment, out_moment, ffn_moment, down_moment, gain_moment)
    averages = (table_average, attn_average, out_average, ffn_average, down_average, gain_average)
    lowered = tuple((member.astype(jnp.bfloat16) for member in masters))
    table_full, attn_full, out_full, ffn_full, down_full, gain_full = (
        lax.all_gather(lowered[0], "dp", axis=0, tiled=True),
        lax.all_gather(lowered[1], "dp", axis=1, tiled=True),
        lax.all_gather(lowered[2], "dp", axis=1, tiled=True),
        lax.all_gather(lowered[3], "dp", axis=1, tiled=True),
        lax.all_gather(lowered[4], "dp", axis=1, tiled=True),
        lax.all_gather(lowered[5], "dp", axis=1, tiled=True),
    )
    gain_values = gain_full.astype(jnp.float32)
    tokens = token_ids[0]
    targets = target_ids[0]
    segments = segment_ids[0]
    domains = domain_ids[0]
    length = tokens.shape[0]
    vocab_rows = table_full.shape[0]
    shard_rows = table.shape[0]
    groups = lax.axis_size("mp")
    member = lax.axis_index("mp")
    matches = (domains[:, None] == jnp.arange(DOMAINS, dtype=jnp.int32)[None, :]).astype(
        jnp.float32
    )
    counts = jnp.maximum(lax.psum(jnp.sum(matches, axis=0), "dp"), 1.0)
    inside, local_ids = owned_rows(tokens, shard_rows, groups, member)
    picked = jnp.take(table_full, jnp.clip(local_ids, 0, vocab_rows - 1), axis=0).astype(
        jnp.float32
    )
    embedded = lax.psum(jnp.where(inside[:, None], picked, 0.0).astype(jnp.bfloat16), "mp").astype(
        jnp.float32
    )
    cosine, sine = rotary_tables(length, HD // 2)
    first_in, first_factor = normed(embedded, gain_values[0])
    attn_in, attn_factor = normed(embedded, gain_values[1])
    first_low = first_in.astype(jnp.bfloat16)
    attn_low = attn_in.astype(jnp.bfloat16)
    value_first = jnp.dot(first_low, attn_full[3], preferred_element_type=jnp.float32).astype(
        jnp.bfloat16
    )
    projected = jnp.einsum(
        "td,kdc->ktc", attn_low, attn_full[:3], preferred_element_type=jnp.float32
    )
    local_heads = attn_full.shape[2] // HD
    queries = rotate(projected[0].reshape(length, local_heads, HD), cosine, sine, 1.0).astype(
        jnp.bfloat16
    )
    keys = rotate(projected[1].reshape(length, local_heads, HD), cosine, sine, 1.0).astype(
        jnp.bfloat16
    )
    values = (
        (0.5 * projected[2] + 0.5 * value_first.astype(jnp.float32))
        .astype(jnp.bfloat16)
        .reshape(length, local_heads, HD)
    )
    block_rows = min(512, length)
    mixed, log_totals = attend_forward(queries, keys, values, segments, block_rows)
    mixed_low = mixed.reshape(length, local_heads * HD).astype(jnp.bfloat16)
    residual_one = embedded + lax.psum(
        jnp.dot(mixed_low, out_full, preferred_element_type=jnp.float32), "mp"
    )
    ffn_in, ffn_factor = normed(residual_one, gain_values[2])
    ffn_low = ffn_in.astype(jnp.bfloat16)
    gate_up = jnp.einsum("td,kdf->ktf", ffn_low, ffn_full, preferred_element_type=jnp.float32)
    sigmoid_gate = jax.nn.sigmoid(gate_up[0])
    silu_gate = gate_up[0] * sigmoid_gate
    activated = (silu_gate * gate_up[1]).astype(jnp.bfloat16)
    residual_two = residual_one + lax.psum(
        jnp.dot(activated, down_full, preferred_element_type=jnp.float32), "mp"
    )
    final_in, final_factor = normed(residual_two, gain_values[3])
    final_low = final_in.astype(jnp.bfloat16)
    logits = contract_last(final_low, table_full)
    target_inside, target_local = owned_rows(targets, shard_rows, groups, member)
    target_hits = (
        jnp.arange(vocab_rows, dtype=jnp.int32)[None, :] == target_local[:, None]
    ) & target_inside[:, None]
    target_logit = jnp.sum(jnp.where(target_hits, logits, 0.0), axis=-1)
    row_high = lax.pmax(jnp.max(logits, axis=-1), "mp")
    row_total, target_total = lax.psum(
        (jnp.sum(jnp.exp(logits - row_high[:, None]), axis=-1), target_logit), "mp"
    )
    row_lse = row_high + jnp.log(row_total)
    token_loss = row_lse - target_total
    domain_sums = lax.psum(jnp.sum(matches * token_loss[:, None], axis=0), "dp")
    weight_values = domain_weights.astype(jnp.float32)
    total_weight = jnp.sum(weight_values)
    domain_loss = domain_sums / counts
    total_loss = jnp.sum(weight_values * domain_loss) / total_weight
    token_coef = jnp.sum(matches * (weight_values / total_weight / counts)[None, :], axis=1)
    logit_grad = (
        (jnp.exp(logits - row_lse[:, None]) - target_hits.astype(jnp.float32)) * token_coef[:, None]
    ).astype(jnp.bfloat16)
    table_head = contract_rows(logit_grad, final_low)
    final_grad = lax.psum(jnp.dot(logit_grad, table_full, preferred_element_type=jnp.float32), "mp")
    two_grad, final_gain = normed_back(residual_two, final_factor, gain_values[3], final_grad)
    down_in = two_grad.astype(jnp.bfloat16)
    down_grad = contract_rows(activated, down_in)
    act_grad = contract_last(down_in, down_full)
    gate_grad = act_grad * gate_up[1] * sigmoid_gate * (1.0 + gate_up[0] * (1.0 - sigmoid_gate))
    pair_grad = jnp.stack([gate_grad, act_grad * silu_gate]).astype(jnp.bfloat16)
    ffn_grad = jnp.einsum("td,ktf->kdf", ffn_low, pair_grad, preferred_element_type=jnp.float32)
    ffn_back = lax.psum(
        jnp.einsum("ktf,kdf->td", pair_grad, ffn_full, preferred_element_type=jnp.float32), "mp"
    )
    ffn_inward, ffn_gain = normed_back(residual_one, ffn_factor, gain_values[2], ffn_back)
    one_grad = two_grad + ffn_inward
    attn_out = one_grad.astype(jnp.bfloat16)
    out_grad = contract_rows(mixed_low, attn_out)
    mixed_grad = (
        contract_last(attn_out, out_full).astype(jnp.bfloat16).reshape(length, local_heads, HD)
    )
    query_grad, key_grad, value_grad = attend_backward(
        queries, keys, values, segments, log_totals, mixed_grad, block_rows
    )
    half_value = (value_grad * 0.5).astype(jnp.bfloat16).reshape(length, local_heads * HD)
    query_raw = (
        rotate(query_grad, cosine, sine, -1.0)
        .reshape(length, local_heads * HD)
        .astype(jnp.bfloat16)
    )
    key_raw = (
        rotate(key_grad, cosine, sine, -1.0).reshape(length, local_heads * HD).astype(jnp.bfloat16)
    )
    triple_grad = jnp.stack([query_raw, key_raw, half_value])
    attn_grad = jnp.concatenate(
        [
            jnp.einsum("td,ktc->kdc", attn_low, triple_grad, preferred_element_type=jnp.float32),
            contract_rows(first_low, half_value)[None],
        ],
        axis=0,
    )
    attn_back, first_back = (
        lax.psum(
            jnp.einsum(
                "ktc,kdc->td", triple_grad, attn_full[:3], preferred_element_type=jnp.float32
            ).astype(jnp.bfloat16),
            "mp",
        ).astype(jnp.float32),
        lax.psum(contract_last(half_value, attn_full[3]).astype(jnp.bfloat16), "mp").astype(
            jnp.float32
        ),
    )
    attn_inward, attn_gain = normed_back(embedded, attn_factor, gain_values[1], attn_back)
    first_inward, first_gain = normed_back(embedded, first_factor, gain_values[0], first_back)
    embed_grad = one_grad + attn_inward + first_inward
    embed_ids = jnp.where(inside, local_ids, vocab_rows)
    gain_grad = jnp.stack([first_gain, attn_gain, ffn_gain, final_gain])
    table_grad = table_head + jax.ops.segment_sum(embed_grad, embed_ids, num_segments=vocab_rows)
    summed = (
        lax.psum_scatter(table_grad, "dp", scatter_dimension=0, tiled=True),
        lax.psum_scatter(attn_grad, "dp", scatter_dimension=1, tiled=True),
        lax.psum_scatter(out_grad, "dp", scatter_dimension=1, tiled=True),
        lax.psum_scatter(ffn_grad, "dp", scatter_dimension=1, tiled=True),
        lax.psum_scatter(down_grad, "dp", scatter_dimension=1, tiled=True),
        lax.psum_scatter(gain_grad, "dp", scatter_dimension=1, tiled=True),
    )
    gain_share = jnp.where(member == 0, 1.0, 0.0)
    squares = sum((jnp.sum(part * part) for part in summed[:5])) + gain_share * jnp.sum(
        summed[5] * summed[5]
    )
    grad_norm = jnp.sqrt(lax.psum(squares, ("dp", "mp")))
    clip_factor = jnp.minimum(1.0, CLIP_NORM / grad_norm)
    results = [total_loss, domain_loss, grad_norm]
    for master, moment, average, gradient in zip(masters, moments, averages, summed):
        clipped = gradient * clip_factor
        new_moment = MOMENTUM * moment + clipped
        new_weight = master - LEARN_RATE * (clipped + MOMENTUM * new_moment)
        results.extend(
            [new_moment, new_weight, AVERAGE_KEEP * average + (1.0 - AVERAGE_KEEP) * new_weight]
        )
    return tuple(results)


def solution(mesh):
    return jax.shard_map(
        per_device,
        mesh=mesh,
        in_specs=(
            P("dp", None),
            P("dp", None),
            P("dp", None),
            P("dp", None),
            P(),
            P(("dp", "mp"), None),
            P(None, "dp", "mp"),
            P("mp", "dp"),
            P(None, "dp", "mp"),
            P("mp", "dp"),
            P(None, "dp"),
            P(("dp", "mp"), None),
            P(None, "dp", "mp"),
            P("mp", "dp"),
            P(None, "dp", "mp"),
            P("mp", "dp"),
            P(None, "dp"),
            P(("dp", "mp"), None),
            P(None, "dp", "mp"),
            P("mp", "dp"),
            P(None, "dp", "mp"),
            P("mp", "dp"),
            P(None, "dp"),
        ),
        out_specs=(
            P(),
            P(),
            P(),
            P(("dp", "mp"), None),
            P(("dp", "mp"), None),
            P(("dp", "mp"), None),
            P(None, "dp", "mp"),
            P(None, "dp", "mp"),
            P(None, "dp", "mp"),
            P("mp", "dp"),
            P("mp", "dp"),
            P("mp", "dp"),
            P(None, "dp", "mp"),
            P(None, "dp", "mp"),
            P(None, "dp", "mp"),
            P("mp", "dp"),
            P("mp", "dp"),
            P("mp", "dp"),
            P(None, "dp"),
            P(None, "dp"),
            P(None, "dp"),
        ),
        check_vma=False,
    )
```

profile of v0, /device:TPU:12, one launch (start us, length us, event | category | flops | bytes accessed | tf_op | source)
XLA Modules:
  0.0 2832.7 jit_solution(4468317093372477944)
XLA Ops:
  13.2 493.0 %all-gather.12.cloned.1.call-done = bf16[8,1572,1024]{2,1,0:T(8,128)(2,1)} async-done(((bf16[1,1572,1024]{2,1,0:T(8,128)(2,1)}), bf16[8,1572,1024]{2,1,0:T(8,128)(2,1)}) %all-gather.12.cloned.1.call-update) | async-done | bytes 25755664 | tf_op jit(solution)/shard_map/all_gather | solution.py:166
  506.2 27.0 reshape.579
  533.2 16.6 gather_fusion
  553.1 16.9 all_gather.19
  570.1 30.8 %all_gather.21 = bf16[256,1024]{1,0:T(8,128)(2,1)} all-gather(bf16[256,128]{1,0:T(8,128)(2,1)S(1)} %convert_element_type.145), channel_id=1, replica_groups=mesh['dp'=8,'mp'=4] {'dp'}, dimensions={1}, use_global_device_ids=true | all-gather | bytes 589824 | tf_op jit(solution)/shard_map/all_gather | solution.py:168
  605.3 49.4 %all-gather.6.cloned.1.call-done = bf16[4,1024,256]{1,2,0:T(8,128)(2,1)} async-done(((bf16[4,128,256]{1,2,0:T(8,128)(2,1)}), bf16[4,1024,256]{1,2,0:T(8,128)(2,1)}) %all-gather.6.cloned.1.call-update) | async-done | bytes 2097168 | tf_op jit(solution)/shard_map/all_gather | solution.py:167
  663.0 23.4 while.27
  696.2 81.7 %all-reduce.13.cloned.1.call-done = f32[1024,1024]{1,0:T(8,128)} async-done(((f32[1024,1024]{1,0:T(8,128)}), f32[1024,1024]{1,0:T(8,128)}) %all-reduce.13.cloned.1.call-update) | async-done | bytes 4194320 | tf_op jit(solution)/shard_map/psum | solution.py:220
  783.2 55.8 %all-gather.8.cloned.1.call-done = bf16[2,1024,704]{1,2,0:T(8,128)(2,1)} async-done(((bf16[2,128,704]{1,2,0:T(8,128)(2,1)}), bf16[2,1024,704]{1,2,0:T(8,128)(2,1)}) %all-gather.8.cloned.1.call-update) | async-done | bytes 2883600 | tf_op jit(solution)/shard_map/all_gather | solution.py:169
  839.0 7.1 convolution_bitcast_fusion.1
  849.6 34.0 %all-gather.10.cloned.1.call-done = bf16[704,1024]{1,0:T(8,128)(2,1)} async-done(((bf16[704,128]{1,0:T(8,128)(2,1)}), bf16[704,1024]{1,0:T(8,128)(2,1)}) %all-gather.10.cloned.1.call-update) | async-done | bytes 1441808 | tf_op jit(solution)/shard_map/all_gather | solution.py:170
  889.6 16.9 psum.90
  907.8 65.0 %all-reduce.15.cloned.1.call-done = f32[1024,1024]{1,0:T(8,128)} async-done(((f32[1024,1024]{1,0:T(8,128)}), f32[1024,1024]{1,0:T(8,128)}) %all-reduce.15.cloned.1.call-update) | async-done | bytes 4194320 | tf_op jit(solution)/shard_map/psum | solution.py:229
  978.8 37.3 %fusion.106 = (f32[1024]{0:T(1024)S(1)}, f32[1024,12576]{0,1:T(8,128)}) fusion(bf16[12576,1024]{1,0:T(8,128)(2,1)} %reshape.579, f32[1024,1024]{1,0:T(8,128)} %get-tuple-element.345, f32[1024]{0:T(1024)S(1)} %bitcast.211, f32[1024]{0:T(1024)S(1)} %get-tuple-element.382), kind=kOutput, calls=%fused_computation.254 | convolution fusion | flops 26389807104 | bytes 81473536 | tf_op jit(solution)/shard_map/dot_general | solution.py:124
  1016.1 6.1 pmax.7
  1022.2 24.7 select_reduce_fusion
  1046.9 6.3 all-reduce.2
  1053.8 44.8 %fusion.101 = f32[1024,1024]{1,0:T(8,128)} fusion(bf16[12576,1024]{1,0:T(8,128)(2,1)} %reshape.579, f32[1024,12576]{0,1:T(8,128)} %get-tuple-element.389, f32[1024]{0:T(1024)S(1)} %get-tuple-element.273, f32[1024]{0:T(1024)S(1)} %get-tuple-element.343, s32[1024]{0:T(1024)S(1)} %fusion.91, pred[1024]{0:T(1024)(128)(4,1)S(1)} %fusion.92), kind=kOutput, calls=%fused_computation.250 | convolution fusion | flops 26463928320 | bytes 81474560 | tf_op jit(solution)/shard_map/dot_general | solution.py:256
  1098.7 85.7 %all-reduce.17.cloned.1.call-done = f32[1024,1024]{1,0:T(8,128)} async-done(((f32[1024,1024]{1,0:T(8,128)}), f32[1024,1024]{1,0:T(8,128)}) %all-reduce.17.cloned.1.call-update) | async-done | bytes 4194320 | tf_op jit(solution)/shard_map/psum | solution.py:256
  1202.2 85.7 %all-reduce.19.cloned.1.call-done = f32[1024,1024]{1,0:T(8,128)} async-done(((f32[1024,1024]{1,0:T(8,128)}), f32[1024,1024]{1,0:T(8,128)}) %all-reduce.19.cloned.1.call-update) | async-done | bytes 4194320 | tf_op jit(solution)/shard_map/psum | solution.py:264
  1300.5 68.7 %while.28 = (s32[]{:T(128)}, f32[1024,4,64]{0,2,1:T(8,128)S(1)}, f32[1024,4,64]{0,2,1:T(8,128)}, f32[2,512,4,64]{1,0,3,2:T(2,128)}, s32[2]{0:T(128)S(1)}, /*inde...) while((s32[]{:T(128)}, f32[1024,4,64]{0,2,1:T(8,128)S(1)}, ...), condition=%wide.region_29.30_spmd.clone, body=%wide.region_27.29_spmd.clone.sunk | while | flops 1376647680 | bytes 164698512 | solution.py:113
  1315.4 10.4 dynamic_update_slice.19
  1349.0 10.4 dynamic_update_slice.19
  1386.7 80.8 %all-reduce.21.cloned.1.call-done = (bf16[1024,1024]{1,0:T(8,128)(2,1)}, bf16[1024,1024]{1,0:T(8,128)(2,1)}) async-done(((bf16[1024,1024]{1,0:T(8,128)(2,1)}, bf16[1024,1024]{1,0:T(8,128)(2,1)}), (bf16[1024,1024]{1,0:T(8,128)(2,1)}, bf16[1024,1024]{1,0:T(8,128)(2,1)})) %all-reduce.21.cloned.1.call-update) | async-done | bytes 4194320 | tf_op jit(solution)/shard_map/psum | solution.py:301
  1488.6 18.9 psum.89
  1507.6 45.8 %fusion.99 = f32[12576,1024]{1,0:T(8,128)} fusion(f32[1024,1024]{1,0:T(8,128)} %get-tuple-element.345, f32[1024]{0:T(1024)S(1)} %bitcast.214, f32[1024]{0:T(1024)S(1)} %copy-done.62, f32[1024,12576]{0,1:T(8,128)} %get-tuple-element.389, f32[1024]{0:T(1024)S(1)} %copy-done.88, f32[1024]{0:T(1024)S(1)} %copy-done.86, s32[1024]{0:T(1024)S(1)} %copy-done.80, ...), kind=kOutput, calls=%fused_computation.248 | convolution fusion | flops 26467074048 | bytes 107238400 | tf_op jit(solution)/shard_map/dot_general | solution.py:118
  1553.4 8.9 convolution_bitcast_fusion
  1569.0 43.6 %scatter_fusion = f32[12576,1024]{1,0:T(8,128)} fusion(f32[12576,1024]{1,0:T(8,128)} %fusion.99, s32[1024]{0:T(1024)S(1)} %bitcast.227, f32[1024,1024]{1,0:T(8,128)} %fusion.47), kind=kCustom, calls=%fused_computation.1 | custom fusion | flops 1048576 | bytes 12587008 | tf_op jit(solution)/shard_map/scatter-add | solution.py:310
  1612.5 1083.3 %fusion = f32[1584,1024]{1,0:T(8,128)} fusion(f32[12576,1024]{1,0:T(8,128)} %scatter_fusion), kind=kCustom, calls=%all-reduce-scatter | all-reduce-scatter fusion | flops 12976129 | bytes 57999872
  2708.4 18.1 concatenate.24
  2741.6 56.3 %psum.95 = f32[]{:T(128)} all-reduce(f32[]{:T(128)S(6)} %add.415), channel_id=1, replica_groups=mesh['dp'=8,'mp'=4] {'dp','mp'}, use_global_device_ids=true, to_apply=%region_51.52 | all-reduce | flops 1 | bytes 8 | tf_op jit(solution)/shard_map/psum | solution.py:323
  2803.5 16.7 multiply_add_fusion
  (402 shorter events, 222.0 us)
Async XLA Ops:
  7.2 499.0 %all-gather.12.cloned.1.call-start = ((), (), s32[]{:S(2)}) async-start(), calls=%async_computation.17 | async-start | bytes 29048832 | tf_op jit(solution)/shard_map/all_gather | solution.py:166
  12.3 590.3 %all-reduce.11.cloned.1.call-start = ((), (), s32[]{:S(2)}) async-start(), calls=%async_computation.5 | async-start | bytes 4194304 | tf_op jit(solution)/shard_map/psum | solution.py:191
  551.9 102.8 %all-gather.6.cloned.1.call-start = ((), (), s32[]{:S(2)}) async-start(), calls=%async_computation.6 | async-start | bytes 2359296 | tf_op jit(solution)/shard_map/all_gather | solution.py:167
  552.2 106.5 %copy-start.24 = (f32[4,128,256]{1,2,0:T(8,128)}, f32[4,128,256]{1,2,0:T(8,128)S(1)}, u32[]{:S(2)}) copy-start(f32[4,128,256]{1,2,0:T(8,128)S(1)} %copy.87) | copy-start | bytes 1572868
  553.0 224.9 %all-reduce.13.cloned.1.call-start = ((), (), s32[]{:S(2)}) async-start(), calls=%async_computation.7 | async-start | bytes 8388608 | tf_op jit(solution)/shard_map/psum | solution.py:220
  570.1 88.6 %copy-start.72 = (f32[1,1024]{1,0:T(1,128)}, f32[1,1024]{1,0:T(1,128)S(1)}, u32[]{:S(2)}) copy-start(f32[1,1024]{1,0:T(1,128)S(1)} %get-tuple-element.376) | copy-start | bytes 12292
  570.1 89.3 %copy-start.70 = (f32[1,1024]{1,0:T(1,128)}, f32[1,1024]{1,0:T(1,128)S(1)}, u32[]{:S(2)}) copy-start(f32[1,1024]{1,0:T(1,128)S(1)} %get-tuple-element.375) | copy-start | bytes 12292
  570.1 269.0 %copy-start.63 = (f32[1,1024]{1,0:T(1,128)}, f32[1,1024]{1,0:T(1,128)S(1)}, u32[]{:S(2)}) copy-start(f32[1,1024]{1,0:T(1,128)S(1)} %get-tuple-element.374) | copy-start | bytes 12292
  570.1 619.0 %copy-start.66 = (f32[1,1024]{1,0:T(1,128)}, f32[1,1024]{1,0:T(1,128)S(1)}, u32[]{:S(2)}) copy-start(f32[1,1024]{1,0:T(1,128)S(1)} %get-tuple-element.373) | copy-start | bytes 12292
  693.0 146.0 %all-gather.8.cloned.1.call-start = ((), (), s32[]{:S(2)}) async-start(), calls=%async_computation.8 | async-start | bytes 3244032 | tf_op jit(solution)/shard_map/all_gather | solution.py:169
  694.9 188.6 %all-gather.10.cloned.1.call-start = ((), (), s32[]{:S(2)}) async-start(), calls=%async_computation.9 | async-start | bytes 1622016 | tf_op jit(solution)/shard_map/all_gather | solution.py:170
  695.7 277.1 %all-reduce.15.cloned.1.call-start = ((), (), s32[]{:S(2)}) async-start(), calls=%async_computation.10 | async-start | bytes 8388608 | tf_op jit(solution)/shard_map/psum | solution.py:229
  888.8 295.6 %all-reduce.17.cloned.1.call-start = ((), (), s32[]{:S(2)}) async-start(), calls=%async_computation.11 | async-start | bytes 8388608 | tf_op jit(solution)/shard_map/psum | solution.py:256
  907.8 146.0 %copy-start.83 = (pred[1024]{0:T(1024)(128)(4,1)}, pred[1024]{0:T(1024)(128)(4,1)S(1)}, u32[]{:S(2)}) copy-start(pred[1024]{0:T(1024)(128)(4,1)S(1)} %fusion.92) | copy-start | bytes 3076
  907.8 146.0 %copy-start.79 = (s32[1024]{0:T(1024)}, s32[1024]{0:T(1024)S(1)}, u32[]{:S(2)}) copy-start(s32[1024]{0:T(1024)S(1)} %fusion.91) | copy-start | bytes 12292
  978.8 210.3 %copy-start.61 = (f32[1024]{0:T(1024)}, f32[1024]{0:T(1024)S(1)}, u32[]{:S(2)}) copy-start(f32[1024]{0:T(1024)S(1)} %get-tuple-element.382) | copy-start | bytes 12292
  1098.6 189.2 %all-reduce.19.cloned.1.call-start = ((), (), s32[]{:S(2)}) async-start(), calls=%async_computation.12 | async-start | bytes 8388608 | tf_op jit(solution)/shard_map/psum | solution.py:264
  1202.0 85.8 %copy-start.59 = (f32[1024]{0:T(1024)S(1)}, f32[1024]{0:T(1024)}, u32[]{:S(2)}) copy-start(f32[1024]{0:T(1024)} %copy-done.58) | copy-start | bytes 12292
  1202.0 85.8 %copy-start.64 = (f32[1,1024]{1,0:T(1,128)S(1)}, f32[1,1024]{1,0:T(1,128)}, u32[]{:S(2)}) copy-start(f32[1,1024]{1,0:T(1,128)} %copy-done.63) | copy-start | bytes 12292
  1202.1 265.5 %all-reduce.21.cloned.1.call-start = ((), (), s32[]{:S(2)}) async-start(), calls=%async_computation.19 | async-start | bytes 8388608 | tf_op jit(solution)/shard_map/psum | solution.py:301
  1202.2 90.4 %copy-start.74 = (f32[1024]{0:T(1024)S(1)}, f32[1024]{0:T(1024)}, u32[]{:S(2)}) copy-start(f32[1024]{0:T(1024)} %get-tuple-element.379) | copy-start | bytes 12292
  1381.8 85.8 %copy-start.11 = (bf16[1024,1024]{1,0:T(8,128)(2,1)S(1)}, bf16[1024,1024]{1,0:T(8,128)(2,1)}, u32[]{:S(2)}) copy-start(bf16[1024,1024]{1,0:T(8,128)(2,1)} %all-reduce.11.cloned.1.call-done) | copy-start | bytes 6291460
  1381.8 85.8 %copy-start.69 = (f32[1024]{0:T(1024)S(1)}, f32[1024]{0:T(1024)}, u32[]{:S(2)}) copy-start(f32[1024]{0:T(1024)} %copy-done.68) | copy-start | bytes 12292
  1381.8 85.8 %copy-start.71 = (f32[1,1024]{1,0:T(1,128)S(1)}, f32[1,1024]{1,0:T(1,128)}, u32[]{:S(2)}) copy-start(f32[1,1024]{1,0:T(1,128)} %copy-done.70) | copy-start | bytes 12292
  1381.8 1319.7 %reduce-scatter.12.cloned.1.call-start = ((), (), s32[]{:S(2)}) async-start(), calls=%async_computation.14 | async-start | bytes 1179648 | tf_op jit(solution)/shard_map/reduce_scatter | solution.py:314
  1386.7 1316.4 %reduce-scatter.18.cloned.1.call-start = ((), (), s32[]{:S(2)}) async-start(), calls=%async_computation.18 | async-start | bytes 589824
  1473.3 1258.3 %reduce-scatter.16.cloned.1.call-start = ((), (), s32[]{:S(2)}) async-start(), calls=%async_computation.16 | async-start | bytes 3244032 | tf_op jit(solution)/shard_map/reduce_scatter | solution.py:316
  1479.2 1254.1 %reduce-scatter.10.cloned.1.call-start = ((), (), s32[]{:S(2)}) async-start(), calls=%async_computation.13 | async-start | bytes 4718592 | tf_op jit(solution)/shard_map/reduce_scatter | solution.py:313
  1485.0 1252.1 %reduce-scatter.14.cloned.1.call-start = ((), (), s32[]{:S(2)}) async-start(), calls=%async_computation.15 | async-start | bytes 6488064 | tf_op jit(solution)/shard_map/reduce_scatter | solution.py:315
  1612.5 1087.8 %copy-start.90 = (s32[8]{0:T(128)S(1)}, s32[8]{0:T(128)}, u32[]{:S(2)}) copy-start(s32[8]{0:T(128)} %param.31) | copy-start | bytes 100
  1612.5 1087.8 %copy-start.92 = (f32[8]{0:T(128)S(1)}, f32[8]{0:T(128)}, u32[]{:S(2)}) copy-start(f32[8]{0:T(128)} %copy-done.91) | copy-start | bytes 100
  2696.9 11.5 collective-permute-start
  (96 other events, 1488.4 us)
Sparse Core Ops, SparseCore 0:
  12.4 493.7 all-gather.11
  552.0 50.5 all-reduce.10
  605.2 49.3 all-gather.5
  693.1 84.7 all-reduce.12
  780.4 58.6 all-gather.7
  841.5 42.0 all-gather.9
  888.9 83.8 all-reduce.14
  1098.7 85.6 all-reduce.16
  1202.2 85.6 all-reduce.18
  1381.9 85.6 all-reduce.20
  1471.0 65.3 reduce-scatter.11
  1540.1 61.5 reduce-scatter.17
  1605.3 178.4 reduce-scatter.15
  1787.2 171.4 reduce-scatter.9
  1962.8 200.6 reduce-scatter.13
where the time goes:
time: 2840 us; the launch traced here: 2830 us
  blocking collectives  1240 us (44%)
  waiting for transfers between devices  1040 us (37%)
  matrix products  228 us (8%)
  other arithmetic  175 us (6%)
  local copies, waits for them, and re-layouts  122 us (4%)
    unnamed x1, blocking collectives  1080 us
    all_gather x1, waiting for transfers between devices, per_device(): lax.all_gather(lowered[0], 'dp', axis=0, tiled=True)  493 us
    psum x1, waiting for transfers between devices, per_device(): lax.psum(jnp.dot(logit_grad, table_full, preferred_element_type=jnp.float...  85.7 us
    psum x1, waiting for transfers between devices, per_device(): lax.psum(jnp.einsum('ktf,kdf->td', pair_grad, ffn_full, preferred_element...  85.7 us
    psum x1, waiting for transfers between devices, per_device(): lax.psum(jnp.dot(mixed_low, out_full, preferred_element_type=jnp.float32)...  81.7 us
    psum x1, waiting for transfers between devices, per_device(): lax.psum(contract_last(half_value, attn_full[3]).astype(jnp.bfloat16), 'mp')  80.8 us
    unnamed x209, local copies, waits for them, and re-layouts  69.6 us
    psum x1, waiting for transfers between devices, per_device(): lax.psum(jnp.dot(activated, down_full, preferred_element_type=jnp.float32...  65 us
  transfers between devices with their start and end apart: 16, of which 11 were waited for; matrix products, arithmetic and copies ran while one was open for 45% of the time, Pallas kernels for 0%

commit v1 on v0

v1 whole, which is shorter than its diff:
```python
import functools

import jax
import jax.numpy as jnp
from jax import lax
from jax.experimental import pallas as pl
from jax.experimental.pallas import tpu as pltpu
from jax.sharding import PartitionSpec as P

HD = 64
DOMAINS = 8
SLOTS = 64

EPSILON = 1e-06
CLIP_NORM = 0.01
LEARN_RATE = 1000.0
MOMENTUM = 0.9
AVERAGE_KEEP = 0.75
MASKED = -1e30
MESH = pl.DeviceIdType.MESH
F32 = jnp.float32
BF16 = jnp.bfloat16
VMEM_SPEC = pl.BlockSpec(memory_space=pltpu.VMEM)
ANY_SPEC = pl.BlockSpec(memory_space=pl.ANY)


def rotary_tables(length, half):
    places = jnp.arange(length, dtype=F32)[:, None]
    speeds = 10000.0 ** (-jnp.arange(half, dtype=F32) / half)
    angles = places * speeds
    return (jnp.cos(angles)[:, None, :], jnp.sin(angles)[:, None, :])


def rotate(values, cosine, sine, direction):
    half = values.shape[-1] // 2
    first = values[..., :half]
    second = values[..., half:]
    return jnp.concatenate(
        [first * cosine - direction * second * sine, second * cosine + direction * first * sine],
        axis=-1,
    )


def block_scores(queries, keys, segments, offset, block_rows):
    query_block = lax.dynamic_slice_in_dim(queries, offset, block_rows, 0)
    query_segments = lax.dynamic_slice_in_dim(segments, offset, block_rows, 0)
    places = jnp.arange(segments.shape[0], dtype=jnp.int32)
    query_places = offset + jnp.arange(block_rows, dtype=jnp.int32)
    allowed = (query_places[:, None] >= places[None, :]) & (
        query_segments[:, None] == segments[None, :]
    )
    raw_scores = jnp.einsum(
        "qhd,khd->hqk", query_block, keys, preferred_element_type=F32
    ) * HD ** (-0.5)
    return (jnp.where(allowed[None], raw_scores, MASKED), query_block)


def attend_forward(queries, keys, values, segments, block_rows):
    length = queries.shape[0]

    def one_block(offset):
        scores, query_block = block_scores(queries, keys, segments, offset, block_rows)
        highest = jnp.max(scores, axis=-1, keepdims=True)
        raised = jnp.exp(scores - highest)
        totals = jnp.sum(raised, axis=-1, keepdims=True)
        mixed = jnp.einsum(
            "hqk,khd->qhd", (raised / totals).astype(BF16), values, preferred_element_type=F32
        )
        return (mixed, (highest + jnp.log(totals))[..., 0])

    offsets = jnp.arange(length // block_rows, dtype=jnp.int32) * block_rows
    mixed, log_totals = lax.map(one_block, offsets)
    return (mixed.reshape(length, queries.shape[1], queries.shape[2]), log_totals)


def attend_backward(queries, keys, values, segments, log_totals, out_grad, block_rows):
    length = queries.shape[0]

    def one_block(carry, inputs):
        offset, block_totals = inputs
        key_grad, value_grad = carry
        scores, query_block = block_scores(queries, keys, segments, offset, block_rows)
        grad_block = lax.dynamic_slice_in_dim(out_grad, offset, block_rows, 0)
        soft_probs = jnp.exp(scores - block_totals[..., None])
        prob_grad = jnp.einsum("qhd,khd->hqk", grad_block, values, preferred_element_type=F32)
        inner = jnp.sum(prob_grad * soft_probs, axis=-1, keepdims=True)
        score_grad = (soft_probs * (prob_grad - inner)).astype(BF16)
        query_grad = jnp.einsum(
            "hqk,khd->qhd", score_grad, keys, preferred_element_type=F32
        ) * HD ** (-0.5)
        key_grad = key_grad + jnp.einsum(
            "hqk,qhd->khd", score_grad, query_block, preferred_element_type=F32
        ) * HD ** (-0.5)
        value_grad = value_grad + jnp.einsum(
            "hqk,qhd->khd", soft_probs.astype(BF16), grad_block, preferred_element_type=F32
        )
        return ((key_grad, value_grad), query_grad)

    empty = jnp.zeros(keys.shape, F32)
    offsets = jnp.arange(length // block_rows, dtype=jnp.int32) * block_rows
    (key_grad, value_grad), query_grad = lax.scan(one_block, (empty, empty), (offsets, log_totals))
    return (query_grad.reshape(queries.shape), key_grad, value_grad)


def contract_rows(left, right):
    return lax.dot_general(left, right, (((0,), (0,)), ((), ())), preferred_element_type=F32)


def contract_last(left, right):
    return lax.dot_general(left, right, (((1,), (1,)), ((), ())), preferred_element_type=F32)


def norm_factor(values):
    return lax.rsqrt(jnp.mean(values * values, axis=-1, keepdims=True) + EPSILON)


def norm_back(values, factor, gain, upward):
    gained = gain * upward
    inward = factor * gained - values * (factor * factor * factor) * jnp.mean(
        gained * values, axis=-1, keepdims=True
    )
    return (inward, jnp.sum(upward * values * factor, axis=0, keepdims=True))


def ring_place(member, count):
    odd = lax.rem(member, 2)
    return (1 - odd) * lax.div(member, 2) + odd * (count - 1 - lax.div(member, 2))


def ring_member(place, count):
    back = lax.div(place, count // 2)
    return (1 - back) * (2 * place) + back * (2 * (count - 1 - place) + 1)


def place_block(member, planes):
    return (member % 2) * planes + member // 2


def greet(peers):
    barrier = pltpu.get_barrier_semaphore()
    for peer in peers:
        pl.semaphore_signal(barrier, inc=1, device_id=peer, device_id_type=MESH)
    pl.semaphore_wait(barrier, len(peers))


def send(source, target, send_sem, recv_sem, peer):
    return pltpu.make_async_remote_copy(
        src_ref=source,
        dst_ref=target,
        send_sem=send_sem,
        recv_sem=recv_sem,
        device_id=peer,
        device_id_type=MESH,
    )


def rows_over_mp(name, ident, groups, partials, blocks, vectors, row_fn, outs, sums, gather, tile):
    planes = groups // 2
    count = len(partials)
    if partials:
        rows, width = partials[0].shape[0] // groups, partials[0].shape[1]
    else:
        rows, width = blocks[0].shape
    shaped = [p.reshape(2, planes, rows, width) for p in partials]
    tile = min(tile, rows)

    def body(*refs):
        refs = list(refs)
        take = lambda n: [refs.pop(0) for _ in range(n)]
        part_refs, block_refs, vector_refs = take(count), take(len(blocks)), take(len(vectors))
        out_refs, sum_refs = take(len(outs)), take(sums)
        whole_ref = take(1)[0] if gather else None
        recv_core, recv_plane, send_plane = take(count), take(count), take(count)
        core_sems, plane_sems, near_sems, far_sems = take(4)
        dp = lax.axis_index("dp")
        member = lax.axis_index("mp")
        plane, core = lax.div(member, 2), lax.rem(member, 2)
        partner = (dp, 2 * plane + 1 - core)
        others = [lax.rem(plane + j, planes) for j in range(1, planes)]
        peers = [(dp, 2 * other + core) for other in others]
        greet([partner] + peers)
        copies = []
        for i in range(count):
            copy = send(
                part_refs[i].at[1 - core], recv_core[i], core_sems.at[0, i], core_sems.at[1, i], partner
            )
            copy.start()
            copies.append(copy)
        plane_copies = []
        for i in range(count):
            copies[i].wait_recv()
            for j, other in enumerate(others):

                @pl.loop(0, rows, step=tile)
                def _(r, i=i, j=j, other=other):
                    at = pl.ds(r, tile)
                    send_plane[i][j, at] = (
                        part_refs[i][core, other, at].astype(F32) + recv_core[i][other, at].astype(F32)
                    ).astype(BF16)

                copy = send(
                    send_plane[i].at[j],
                    recv_plane[i].at[j],
                    plane_sems.at[0, i, j],
                    plane_sems.at[1, i, j],
                    peers[j],
                )
                copy.start()
                plane_copies.append(copy)
        for copy in plane_copies:
            copy.wait_recv()
        for ref in sum_refs:
            ref[...] = jnp.zeros_like(ref)

        @pl.loop(0, rows, step=tile)
        def _(r):
            at = pl.ds(r, tile)
            totals = []
            for i in range(count):
                total = part_refs[i][core, plane, at].astype(F32) + recv_core[i][plane, at].astype(F32)
                for j in range(planes - 1):
                    total = total + recv_plane[i][j, at].astype(F32)
                totals.append(total)
            results, sum_parts, gathered = row_fn(
                totals, [ref[at, :] for ref in block_refs], [ref[...] for ref in vector_refs]
            )
            for ref, result in zip(out_refs, results):
                ref[at, :] = result.astype(ref.dtype)
            for ref, part in zip(sum_refs, sum_parts):
                ref[...] += part
            if gather:
                whole_ref[core, plane, at] = gathered.astype(BF16)

        if gather:
            near, far = [], []
            for j in range(planes - 1):
                copy = send(
                    whole_ref.at[core, plane],
                    whole_ref.at[core, plane],
                    far_sems.at[0, j],
                    far_sems.at[1, j],
                    peers[j],
                )
                copy.start()
                far.append(copy)
            for j in range(planes):
                source = lax.rem(plane + planes - j, planes)
                if j:
                    far[j - 1].wait_recv()
                copy = send(
                    whole_ref.at[core, source],
                    whole_ref.at[core, source],
                    near_sems.at[0, j],
                    near_sems.at[1, j],
                    partner,
                )
                copy.start()
                near.append(copy)
            for copy in near:
                copy.wait_recv()
            for copy in near + far:
                copy.wait_send()
        for copy in copies + plane_copies:
            copy.wait_send()

    out_shape = [jax.ShapeDtypeStruct((rows, width), dtype) for dtype in outs]
    out_shape += [jax.ShapeDtypeStruct((1, width), F32)] * sums
    if gather:
        out_shape.append(jax.ShapeDtypeStruct((2, planes, rows, width), BF16))
    far_count = max(planes - 1, 1)
    scratch = [pltpu.VMEM((planes, rows, width), BF16)] * count
    scratch += [pltpu.VMEM((far_count, rows, width), BF16)] * (2 * count)
    scratch += [
        pltpu.SemaphoreType.DMA((2, max(count, 1))),
        pltpu.SemaphoreType.DMA((2, max(count, 1), far_count)),
        pltpu.SemaphoreType.DMA((2, planes)),
        pltpu.SemaphoreType.DMA((2, far_count)),
    ]
    results = pl.pallas_call(
        body,
        name=name,
        out_shape=out_shape,
        in_specs=[VMEM_SPEC] * (count + len(blocks) + len(vectors)),
        out_specs=[VMEM_SPEC] * len(out_shape),
        scratch_shapes=scratch,
        compiler_params=pltpu.CompilerParams(
            collective_id=ident, has_side_effects=True, vmem_limit_bytes=48 * 2**20
        ),
    )(*shaped, *blocks, *vectors)
    results = list(results)
    if gather:
        results[-1] = results[-1].reshape(groups * rows, width)
    return results


def exchange_over_dp(name, ident, values):
    members = values.shape[0]

    def body(in_ref, out_ref, sems):
        dp, mp = lax.axis_index("dp"), lax.axis_index("mp")
        peers = [(lax.rem(dp + k, members), mp) for k in range(1, members)]
        greet(peers)
        copies = []
        for k in range(1, members):
            copy = send(
                in_ref.at[peers[k - 1][0]],
                out_ref.at[dp],
                sems.at[0, k - 1],
                sems.at[1, k - 1],
                peers[k - 1],
            )
            copy.start()
            copies.append(copy)
        out_ref[dp] = in_ref[dp]
        for copy in copies:
            copy.wait_recv()
        for copy in copies:
            copy.wait_send()

    return pl.pallas_call(
        body,
        name=name,
        out_shape=jax.ShapeDtypeStruct(values.shape, values.dtype),
        in_specs=[VMEM_SPEC],
        out_specs=VMEM_SPEC,
        scratch_shapes=[pltpu.SemaphoreType.DMA((2, members - 1))],
        compiler_params=pltpu.CompilerParams(
            collective_id=ident, has_side_effects=True, vmem_limit_bytes=32 * 2**20
        ),
    )(values)


def gather_rows(name, ident, members, groups, block):
    planes = groups // 2
    rows, width = block.shape
    half = planes // 2

    def body(in_ref, out_ref, first_sem, plane_sems, ring_sems, core_sems):
        dp, member = lax.axis_index("dp"), lax.axis_index("mp")
        plane, core = lax.div(member, 2), lax.rem(member, 2)
        place = ring_place(dp, members)
        right = (ring_member(lax.rem(place + 1, members), members), member)
        left = (ring_member(lax.rem(place + members - 1, members), members), member)
        partner = (dp, 2 * plane + 1 - core)
        peers = [(dp, 2 * lax.rem(plane + j, planes) + core) for j in range(1, planes)]
        greet([right, left, partner] + peers)
        own = pltpu.make_async_copy(in_ref, out_ref.at[dp, core, plane], first_sem)
        own.start()
        waits = []
        for j in range(planes - 1):
            copy = send(
                in_ref, out_ref.at[dp, core, plane], plane_sems.at[0, j], plane_sems.at[1, j], peers[j]
            )
            copy.start()
            waits.append(copy)
        own.wait()
        for copy in waits:
            copy.wait_recv()
        ways = ((right, 0, members - 1), (left, 1, 1))

        def piece(source, way):
            return out_ref.at[source, core, pl.ds(way * half, half)]

        def start(k):
            for peer, way, step in ways:
                source = ring_member(lax.rem(place + k * step, members), members)

                @pl.when(k < members - 1)
                def _():
                    send(
                        piece(source, way),
                        piece(source, way),
                        ring_sems.at[0, way, k],
                        ring_sems.at[1, way, k],
                        peer,
                    ).start()

                send(
                    piece(source, way),
                    piece(source, way),
                    core_sems.at[0, way, k],
                    core_sems.at[1, way, k],
                    partner,
                ).start()

        def wait_ring(k):
            for peer, way, step in ways:
                send(
                    piece(dp, way),
                    piece(dp, way),
                    ring_sems.at[0, way, k],
                    ring_sems.at[1, way, k],
                    peer,
                ).wait_recv()

        start(0)

        @pl.loop(1, members)
        def _(k):
            wait_ring(k - 1)
            start(k)

        @pl.loop(0, members)
        def _(k):
            for peer, way, step in ways:
                near = send(
                    piece(dp, way),
                    piece(dp, way),
                    core_sems.at[0, way, k],
                    core_sems.at[1, way, k],
                    partner,
                )
                near.wait_recv()
                near.wait_send()

                @pl.when(k < members - 1)
                def _():
                    send(
                        piece(dp, way),
                        piece(dp, way),
                        ring_sems.at[0, way, k],
                        ring_sems.at[1, way, k],
                        peer,
                    ).wait_send()

        for copy in waits:
            copy.wait_send()

    return pl.pallas_call(
        body,
        name=name,
        out_shape=jax.ShapeDtypeStruct((members, 2, planes, rows, width), block.dtype),
        in_specs=[VMEM_SPEC],
        out_specs=ANY_SPEC,
        scratch_shapes=[
            pltpu.SemaphoreType.DMA,
            pltpu.SemaphoreType.DMA((2, max(planes - 1, 1))),
            pltpu.SemaphoreType.DMA((2, 2, members)),
            pltpu.SemaphoreType.DMA((2, 2, members)),
        ],
        compiler_params=pltpu.CompilerParams(collective_id=ident, has_side_effects=True),
    )(block).reshape(members * groups * rows, width)


def scatter_rows(name, ident, members, groups, values):
    planes = groups // 2
    width = values.shape[1]
    rows = values.shape[0] // (members * groups)
    half = planes // 2
    shaped = values.reshape(members, 2, planes, rows, width)
    tile = min(64, rows)

    def body(
        in_ref,
        out_ref,
        near_ref,
        held,
        going,
        own,
        near,
        last,
        plane_held,
        core_sems,
        ring_sems,
        load_sems,
        plane_sems,
    ):
        dp, member = lax.axis_index("dp"), lax.axis_index("mp")
        plane, core = lax.div(member, 2), lax.rem(member, 2)
        place = ring_place(dp, members)
        right = (ring_member(lax.rem(place + 1, members), members), member)
        left = (ring_member(lax.rem(place + members - 1, members), members), member)
        partner = (dp, 2 * plane + 1 - core)
        others = [lax.rem(plane + j, planes) for j in range(1, planes)]
        peers = [(dp, 2 * other + core) for other in others]
        greet([right, left, partner] + peers)
        ways = ((right, 0, members - 1), (left, 1, 1))

        def target(k, way):
            step = ways[way][2]
            return ring_member(lax.rem(place + (k + 1) * step, members), members)

        def core_copy(k, way):
            block = target(k, way)
            at = pl.ds(way * half, half)
            return send(
                in_ref.at[block, 1 - core, at],
                near_ref.at[block, at],
                core_sems.at[0, way, k],
                core_sems.at[1, way, k],
                partner,
            )

        def loads(k, way):
            block, slot = target(k, way), lax.rem(k, 2)
            at = pl.ds(way * half, half)
            return (
                pltpu.make_async_copy(
                    in_ref.at[block, core, at], own.at[way, slot], load_sems.at[0, way, slot]
                ),
                pltpu.make_async_copy(
                    near_ref.at[block, at], near.at[way, slot], load_sems.at[1, way, slot]
                ),
            )

        def ring_copy(k, way):
            return send(
                going.at[way, lax.rem(k, 2)],
                held.at[way, k],
                ring_sems.at[0, way, k],
                ring_sems.at[1, way, k],
                ways[way][0],
            )

        @pl.loop(0, members)
        def _(k):
            for way in range(2):
                core_copy(k, way).start()

        for way in range(2):
            core_copy(0, way).wait_recv()
            for load in loads(0, way):
                load.start()

        @pl.loop(0, members)
        def _(k):
            slot = lax.rem(k, 2)

            @pl.when(k + 1 < members)
            def _():
                for way in range(2):
                    core_copy(k + 1, way).wait_recv()
                    for load in loads(k + 1, way):
                        load.start()

            for way in range(2):
                for load in loads(k, way):
                    load.wait()

                @pl.when(k >= 2)
                def _():
                    ring_copy(k - 2, way).wait_send()

                @pl.when(k >= 1)
                def _():
                    ring_copy(k - 1, way).wait_recv()

                for b in range(half):

                    @pl.loop(0, rows, step=tile)
                    def _(r):
                        at = pl.ds(r, tile)
                        mine = own[way, slot, b, at].astype(F32) + near[way, slot, b, at].astype(F32)

                        @pl.when(k == 0)
                        def _():
                            going[way, slot, b, at] = mine.astype(BF16)

                        @pl.when(k > 0)
                        def _():
                            came = held[way, jnp.maximum(k - 1, 0), b, at].astype(F32)

                            @pl.when(k < members - 1)
                            def _():
                                going[way, slot, b, at] = (mine + came).astype(BF16)

                            @pl.when(k == members - 1)
                            def _():
                                last[way * half + b, at] = mine + came
                                going[way, slot, b, at] = (mine + came).astype(BF16)

                @pl.when(k < members - 1)
                def _():
                    ring_copy(k, way).start()

        for way in range(2):
            ring_copy(members - 2, way).wait_send()
        final = (members - 1) % 2
        plane_copies = []
        for j, other in enumerate(others):
            copy = send(
                going.at[lax.div(other, half), final, lax.rem(other, half)],
                plane_held.at[j],
                plane_sems.at[0, j],
                plane_sems.at[1, j],
                peers[j],
            )
            copy.start()
            plane_copies.append(copy)

        @pl.loop(0, members)
        def _(k):
            for way in range(2):
                core_copy(k, way).wait_send()

        for copy in plane_copies:
            copy.wait_recv()

        @pl.loop(0, rows, step=tile)
        def _(r):
            at = pl.ds(r, tile)
            total = last[plane, at]
            for j in range(planes - 1):
                total = total + plane_held[j, at].astype(F32)
            out_ref[at, :] = total

        for copy in plane_copies:
            copy.wait_send()

    message = (half, rows, width)
    return pl.pallas_call(
        body,
        name=name,
        out_shape=[
            jax.ShapeDtypeStruct((rows, width), F32),
            jax.ShapeDtypeStruct((members, planes, rows, width), BF16),
        ],
        in_specs=[ANY_SPEC],
        out_specs=[VMEM_SPEC, ANY_SPEC],
        scratch_shapes=[
            pltpu.VMEM((2, members - 1, *message), BF16),
            pltpu.VMEM((2, 2, *message), BF16),
            pltpu.VMEM((2, 2, *message), BF16),
            pltpu.VMEM((2, 2, *message), BF16),
            pltpu.VMEM((planes, rows, width), F32),
            pltpu.VMEM((planes - 1, rows, width), BF16),
            pltpu.SemaphoreType.DMA((2, 2, members)),
            pltpu.SemaphoreType.DMA((2, 2, members - 1)),
            pltpu.SemaphoreType.DMA((2, 2, 2)),
            pltpu.SemaphoreType.DMA((2, planes - 1)),
        ],
        compiler_params=pltpu.CompilerParams(
            collective_id=ident, has_side_effects=True, vmem_limit_bytes=56 * 2**20
        ),
    )(shaped)[0]


def head_forward(hidden, table, places, vocab, tile):
    tokens, width = hidden.shape
    padded = table.shape[0]

    def body(hidden_ref, table_ref, place_ref, raised_ref, high_ref, total_ref, hit_ref):
        logits = contract_last(table_ref[...], hidden_ref[...])
        row = lax.broadcasted_iota(jnp.int32, logits.shape, 0)
        inside = jnp.where(row < vocab, logits, MASKED)
        high = jnp.max(inside, axis=0, keepdims=True)
        raised = jnp.exp(inside - high)
        raised_ref[...] = raised.astype(BF16)
        high_ref[...] = high
        total_ref[...] = jnp.sum(raised, axis=0, keepdims=True)
        hit_ref[...] = jnp.sum(jnp.where(row == place_ref[...], logits, 0.0), axis=0, keepdims=True)

    line = pl.BlockSpec((1, tile), lambda i: (0, i))
    return pl.pallas_call(
        body,
        name="head_forward",
        grid=(tokens // tile,),
        out_shape=[jax.ShapeDtypeStruct((padded, tokens), BF16)]
        + [jax.ShapeDtypeStruct((1, tokens), F32)] * 3,
        in_specs=[
            pl.BlockSpec((tile, width), lambda i: (i, 0)),
            pl.BlockSpec((padded, width), lambda i: (0, 0)),
            line,
        ],
        out_specs=[pl.BlockSpec((padded, tile), lambda i: (0, i)), line, line, line],
        compiler_params=pltpu.CompilerParams(vmem_limit_bytes=58 * 2**20),
    )(hidden, table, places)


def head_backward(raised, scale, coef, places, hidden, table, tile):
    padded, tokens = raised.shape
    width = hidden.shape[1]

    def body(raised_ref, scale_ref, coef_ref, place_ref, hidden_ref, table_ref, back_ref, grad_ref):
        row = lax.broadcasted_iota(jnp.int32, raised_ref.shape, 0)
        hits = jnp.where(row == place_ref[...], coef_ref[...], 0.0)
        slope = (raised_ref[...].astype(F32) * scale_ref[...] - hits).astype(BF16)
        back_ref[...] = contract_rows(slope, table_ref[...]).astype(BF16)
        step = jnp.dot(slope, hidden_ref[...], preferred_element_type=F32)

        @pl.when(pl.program_id(0) == 0)
        def _():
            grad_ref[...] = step

        @pl.when(pl.program_id(0) > 0)
        def _():
            grad_ref[...] += step

    line = pl.BlockSpec((1, tile), lambda i: (0, i))
    return pl.pallas_call(
        body,
        name="head_backward",
        grid=(tokens // tile,),
        out_shape=[
            jax.ShapeDtypeStruct((tokens, width), BF16),
            jax.ShapeDtypeStruct((padded, width), F32),
        ],
        in_specs=[
            pl.BlockSpec((padded, tile), lambda i: (0, i)),
            line,
            line,
            line,
            pl.BlockSpec((tile, width), lambda i: (i, 0)),
            pl.BlockSpec((padded, width), lambda i: (0, 0)),
        ],
        out_specs=[
            pl.BlockSpec((tile, width), lambda i: (i, 0)),
            pl.BlockSpec((padded, width), lambda i: (0, 0)),
        ],
        compiler_params=pltpu.CompilerParams(vmem_limit_bytes=58 * 2**20),
    )(raised, scale, coef, places, hidden, table)


def one_hot(indices, size):
    return (indices[:, None] == jnp.arange(size, dtype=jnp.int32)[None, :]).astype(BF16)


def slots_of(ids, shard):
    length = ids.shape[0]
    owners = ids // shard
    order = jnp.arange(length, dtype=jnp.int32)
    same = ids[:, None] == ids[None, :]
    again = jnp.any(same & (order[None, :] < order[:, None]), axis=1)
    ahead = (owners[:, None] == owners[None, :]) & (ids[None, :] < ids[:, None]) & ~again[None, :]
    return jnp.sum(ahead.astype(jnp.int32), axis=1)


def per_device(
    members,
    groups,
    token_ids,
    target_ids,
    segment_ids,
    domain_ids,
    domain_weights,
    table,
    attn_weights,
    out_weights,
    ffn_weights,
    down_weights,
    gains,
    table_moment,
    attn_moment,
    out_moment,
    ffn_moment,
    down_moment,
    gain_moment,
    table_average,
    attn_average,
    out_average,
    ffn_average,
    down_average,
    gain_average,
):
    masters = (table, attn_weights, out_weights, ffn_weights, down_weights, gains)
    moments = (table_moment, attn_moment, out_moment, ffn_moment, down_moment, gain_moment)
    averages = (table_average, attn_average, out_average, ffn_average, down_average, gain_average)
    planes = groups // 2
    dp, member = lax.axis_index("dp"), lax.axis_index("mp")
    device = dp * groups + member
    block = place_block(member, planes)
    tokens, segments = token_ids[0], segment_ids[0]
    length = tokens.shape[0]
    vocab, width = table.shape
    rows = length // groups
    padded = -(-vocab // 16) * 16

    square = lax.all_gather(
        jnp.concatenate([attn_weights, out_weights.T[None]]).astype(BF16), "dp", axis=1, tiled=True
    )
    long = lax.all_gather(
        jnp.concatenate([ffn_weights, down_weights.T[None]]).astype(BF16), "dp", axis=1, tiled=True
    )
    gain_full = lax.all_gather(gains.astype(BF16), "dp", axis=1, tiled=True).astype(F32)
    gain_rows = [gain_full[i : i + 1] for i in range(4)]
    table_low = jnp.pad(table.astype(BF16), ((0, padded - vocab), (0, 0)))

    slots = slots_of(tokens, vocab)
    known = lax.all_gather(
        jnp.stack([tokens, target_ids[0], domain_ids[0], slots]), "dp", axis=0, tiled=False
    )
    all_ids, all_targets, all_domains, all_slots = (known[:, i] for i in range(4))
    fits = jnp.all(all_slots < SLOTS)
    owners = tokens // vocab
    spots = (
        place_block(owners % groups, planes) * (members * SLOTS) + owners // groups * SLOTS + slots
    )

    def sparse_rows():
        mine = all_ids // vocab == device
        slot = jnp.arange(SLOTS, dtype=jnp.int32)
        wanted = jnp.max(
            jnp.where(
                mine[:, :, None] & (all_slots[:, :, None] == slot), (all_ids % vocab)[:, :, None], -1
            ),
            axis=1,
        ).reshape(-1)
        chosen = jnp.dot(one_hot(wanted, padded), table_low)
        came = exchange_over_dp("embed_dp", 1, chosen.reshape(members, SLOTS, width))
        came = came.reshape(members * SLOTS, width)
        whole = rows_over_mp(
            "embed_mp", 2, groups, [], [came], [], lambda t, b, v: ([], [], b[0]), [], 0, True, 64
        )[0]
        return jnp.dot(one_hot(spots, groups * members * SLOTS), whole)

    def dense_rows():
        flat = all_ids.reshape(-1)
        picked = jnp.take(table_low, flat % vocab, axis=0)
        picked = jnp.where((flat // vocab == device)[:, None], picked, jnp.zeros_like(picked))
        return lax.psum(
            lax.psum_scatter(picked, "dp", scatter_dimension=0, tiled=True), "mp"
        )

    embedded_low = lax.cond(fits, sparse_rows, dense_rows)
    embedded = embedded_low.astype(F32)
    own_rows = lax.dynamic_slice_in_dim(embedded, block * rows, rows, 0)

    cosine, sine = rotary_tables(length, HD // 2)
    factor = norm_factor(embedded)
    first_low = (embedded * factor * gain_rows[0]).astype(BF16)
    attn_low = (embedded * factor * gain_rows[1]).astype(BF16)
    value_first = jnp.dot(first_low, square[3], preferred_element_type=F32).astype(BF16)
    projected = jnp.einsum("td,kdc->ktc", attn_low, square[:3], preferred_element_type=F32)
    columns = square.shape[2]
    heads = columns // HD
    queries = rotate(projected[0].reshape(length, heads, HD), cosine, sine, 1.0).astype(BF16)
    keys = rotate(projected[1].reshape(length, heads, HD), cosine, sine, 1.0).astype(BF16)
    values = (
        (0.5 * projected[2] + 0.5 * value_first.astype(F32)).astype(BF16).reshape(length, heads, HD)
    )
    block_rows = min(512, length)
    mixed, log_totals = attend_forward(queries, keys, values, segments, block_rows)
    mixed_low = mixed.reshape(length, columns).astype(BF16)
    out_part = contract_last(mixed_low, square[4]).astype(BF16)

    def after_attention(totals, blocks, vectors):
        residual = blocks[0] + totals[0]
        return ([residual], [], residual * norm_factor(residual) * vectors[0])

    residual_one, ffn_low = rows_over_mp(
        "after_attention", 3, groups, [out_part], [own_rows], [gain_rows[2]], after_attention,
        [F32], 0, True, 64,
    )

    gate_up = jnp.einsum("td,kdf->ktf", ffn_low, long[:2], preferred_element_type=F32)
    sigmoid_gate = jax.nn.sigmoid(gate_up[0])
    silu_gate = gate_up[0] * sigmoid_gate
    activated = (silu_gate * gate_up[1]).astype(BF16)
    down_part = contract_last(activated, long[2]).astype(BF16)

    def after_ffn(totals, blocks, vectors):
        residual = blocks[0] + totals[0]
        return ([residual, residual * norm_factor(residual) * vectors[0]], [], None)

    residual_two, final_low = rows_over_mp(
        "after_ffn", 4, groups, [down_part], [residual_one], [gain_rows[3]], after_ffn,
        [F32, BF16], 0, False, 64,
    )

    hidden = gather_rows("gather_hidden", 5, members, groups, final_low)
    flat_targets = all_targets.reshape(1, -1)
    places = jnp.where(flat_targets // vocab == device, flat_targets % vocab, -1)
    tile = min(512, length)
    raised, high, total, hit = head_forward(hidden, table_low, places, vocab, tile)
    row_high = lax.pmax(high, ("dp", "mp"))
    row_total, target_total = lax.psum(
        (total * jnp.exp(high - row_high), hit), ("dp", "mp")
    )
    row_lse = row_high + jnp.log(row_total)
    token_loss = (row_lse - target_total)[0]
    matches = (
        all_domains.reshape(-1)[:, None] == jnp.arange(DOMAINS, dtype=jnp.int32)[None, :]
    ).astype(F32)
    counts = jnp.maximum(jnp.sum(matches, axis=0), 1.0)
    domain_loss = jnp.sum(matches * token_loss[:, None], axis=0) / counts
    weight_values = domain_weights.astype(F32)
    total_weight = jnp.sum(weight_values)
    total_loss = jnp.sum(weight_values * domain_loss) / total_weight
    coef = jnp.sum(matches * (weight_values / total_weight / counts)[None, :], axis=1)[None, :]
    scale = coef * jnp.exp(high - row_lse)
    hidden_back, table_head = head_backward(raised, scale, coef, places, hidden, table_low, tile)
    final_grad = scatter_rows("scatter_hidden", 6, members, groups, hidden_back)

    def before_head(totals, blocks, vectors):
        grad, final_gain = norm_back(blocks[1], norm_factor(blocks[1]), vectors[0], blocks[0])
        return ([grad], [final_gain], grad)

    two_grad, final_gain, down_in = rows_over_mp(
        "before_head", 7, groups, [], [final_grad, residual_two], [gain_rows[3]], before_head,
        [F32], 1, True, 64,
    )

    down_grad = contract_rows(down_in, activated)
    act_grad = jnp.dot(down_in, long[2], preferred_element_type=F32)
    gate_grad = act_grad * gate_up[1] * sigmoid_gate * (1.0 + gate_up[0] * (1.0 - sigmoid_gate))
    pair_grad = jnp.stack([gate_grad, act_grad * silu_gate]).astype(BF16)
    ffn_part = jnp.einsum(
        "ktf,kdf->td", pair_grad, long[:2], preferred_element_type=F32
    ).astype(BF16)

    def before_ffn(totals, blocks, vectors):
        inward, ffn_gain = norm_back(blocks[0], norm_factor(blocks[0]), vectors[0], totals[0])
        grad = blocks[1] + inward
        return ([grad], [ffn_gain], grad)

    one_grad, ffn_gain, attn_out = rows_over_mp(
        "before_ffn", 8, groups, [ffn_part], [residual_one, two_grad], [gain_rows[2]], before_ffn,
        [F32], 1, True, 64,
    )
    ffn_grad = jnp.einsum("td,ktf->kdf", ffn_low, pair_grad, preferred_element_type=F32)
    long_sum = lax.psum_scatter(
        jnp.concatenate([ffn_grad, down_grad[None]]).astype(BF16), "dp", scatter_dimension=1, tiled=True
    ).astype(F32)

    out_grad = contract_rows(attn_out, mixed_low)
    mixed_grad = (
        jnp.dot(attn_out, square[4], preferred_element_type=F32).astype(BF16).reshape(length, heads, HD)
    )
    query_grad, key_grad, value_grad = attend_backward(
        queries, keys, values, segments, log_totals, mixed_grad, block_rows
    )
    half_value = (value_grad * 0.5).astype(BF16).reshape(length, columns)
    query_raw = rotate(query_grad, cosine, sine, -1.0).reshape(length, columns).astype(BF16)
    key_raw = rotate(key_grad, cosine, sine, -1.0).reshape(length, columns).astype(BF16)
    triple_grad = jnp.stack([query_raw, key_raw, half_value])
    attn_part = jnp.einsum(
        "ktc,kdc->td", triple_grad, square[:3], preferred_element_type=F32
    ).astype(BF16)
    first_part = contract_last(half_value, square[3]).astype(BF16)

    def before_attention(totals, blocks, vectors):
        factor = norm_factor(blocks[0])
        attn_inward, attn_gain = norm_back(blocks[0], factor, vectors[1], totals[0])
        first_inward, first_gain = norm_back(blocks[0], factor, vectors[0], totals[1])
        return ([], [first_gain, attn_gain], blocks[1] + attn_inward + first_inward)

    first_gain, attn_gain, embed_grad = rows_over_mp(
        "before_attention", 9, groups, [attn_part, first_part], [own_rows, one_grad],
        [gain_rows[0], gain_rows[1]], before_attention, [], 2, True, 64,
    )
    attn_grad = jnp.concatenate(
        [
            jnp.einsum("td,ktc->kdc", attn_low, triple_grad, preferred_element_type=F32),
            contract_rows(first_low, half_value)[None],
            out_grad[None],
        ]
    )
    square_sum = lax.psum_scatter(
        attn_grad.astype(BF16), "dp", scatter_dimension=1, tiled=True
    ).astype(F32)

    def sparse_table():
        first_spot = block * (members * SLOTS)
        places = first_spot + jnp.arange(members * SLOTS, dtype=jnp.int32)
        leaving = jnp.dot(
            (places[:, None] == spots[None, :]).astype(BF16), embed_grad, preferred_element_type=F32
        ).astype(BF16)
        came = exchange_over_dp("table_dp", 10, leaving.reshape(members, SLOTS, width))
        mine = all_ids // vocab == device
        slot = jnp.arange(SLOTS, dtype=jnp.int32)
        wanted = jnp.max(
            jnp.where(
                mine[:, :, None] & (all_slots[:, :, None] == slot), (all_ids % vocab)[:, :, None], -1
            ),
            axis=1,
        ).reshape(-1)
        place = jnp.arange(vocab, dtype=jnp.int32)
        return jnp.dot(
            (place[:, None] == wanted[None, :]).astype(BF16),
            came.reshape(members * SLOTS, width),
            preferred_element_type=F32,
        )

    def dense_table():
        everything = lax.all_gather(embed_grad, "dp", axis=0, tiled=True).astype(F32)
        flat = all_ids.reshape(-1)
        spot = jnp.where(flat // vocab == device, flat % vocab, vocab)
        return jax.ops.segment_sum(everything, spot, num_segments=vocab)

    table_sum = table_head[:vocab] + lax.cond(fits, sparse_table, dense_table)
    gain_grad = lax.psum(
        jnp.concatenate([first_gain, attn_gain, ffn_gain, final_gain]), ("dp", "mp")
    )
    gain_width = gains.shape[1]
    gain_sum = lax.dynamic_slice_in_dim(gain_grad, dp * gain_width, gain_width, 1)
    summed = (table_sum, square_sum[:4], square_sum[4].T, long_sum[:2], long_sum[2].T, gain_sum)
    gain_share = jnp.where(member == 0, 1.0, 0.0)
    squares = sum((jnp.sum(part * part) for part in summed[:5])) + gain_share * jnp.sum(
        summed[5] * summed[5]
    )
    grad_norm = jnp.sqrt(lax.psum(squares, ("dp", "mp")))
    clip_factor = jnp.minimum(1.0, CLIP_NORM / grad_norm)
    results = [total_loss, domain_loss, grad_norm]
    for master, moment, average, gradient in zip(masters, moments, averages, summed):
        clipped = gradient * clip_factor
        new_moment = MOMENTUM * moment + clipped
        new_weight = master - LEARN_RATE * (clipped + MOMENTUM * new_moment)
        results.extend(
            [new_moment, new_weight, AVERAGE_KEEP * average + (1.0 - AVERAGE_KEEP) * new_weight]
        )
    return tuple(results)


def solution(mesh):
    rows = P(("dp", "mp"), None)
    cube = P(None, "dp", "mp")
    down = P("mp", "dp")
    gain = P(None, "dp")
    ids = P("dp", None)
    state = (rows, cube, down, cube, down, gain)
    return jax.shard_map(
        functools.partial(per_device, mesh.shape["dp"], mesh.shape["mp"]),
        mesh=mesh,
        in_specs=(ids, ids, ids, ids, P(), *state, *state, *state),
        out_specs=(P(), P(), P(), *(spec for spec in state for _ in range(3))),
        check_vma=False,
    )
```

time: 2840 us -> 1330 us (0.47)
  blocking collectives: 1240 us -> 171 us
  waiting for transfers between devices: 1040 us -> 244 us
  Pallas kernels: 0 us -> 569 us
  matrix products: 228 us -> 113 us
  other arithmetic: 175 us -> 90.4 us
    unnamed x1 -> x0, blocking collectives: 1080 us -> none
    all_gather x4 -> x2, waiting for transfers between devices: 632 us -> 42.6 us  [the longest x1 35.6 us: per_device(): lax.all_gather(jnp.concatenate([attn_weights, out_weights.T[None]]).astyp...]
    pallas_call x0 -> x12, Pallas kernels: none -> 569 us  [the longest x6 173 us: rows_over_mp(): pl.pallas_call(body, name=name, out_shape=out_shape, in_specs=[VMEM_SPEC]...]
    psum x6 -> x1, waiting for transfers between devices: 400 us -> 120 us  [per_device(): lax.psum((total * jnp.exp(high - row_high), hit), ('dp', 'mp'))]
    unnamed x17 -> x7, waiting for transfers between devices: 3.4 us -> 81.2 us
    reduce_sum x8 -> x2, other arithmetic: 51.4 us -> 2.43 us  [the longest x1 2.25 us: slots_of(): return jnp.sum(ahead.astype(jnp.int32), axis=1)]
    dot_general x4 -> x3, matrix products: 56.4 us -> 8.45 us  [contract_rows(): lax.dot_general(left, right, (((0,), (0,)), ((), ())), preferred_element_...]
    scatter-add x1 -> x0, other arithmetic: 43.6 us -> none  [per_device(): jax.ops.segment_sum(embed_grad, embed_ids, num_segments=vocab_rows)]
  transfers between devices with their start and end apart: 16 -> 5, of which waited for: 11 -> 4; matrix products, arithmetic and copies ran while one was open for 45% -> 6% of each run, Pallas kernels for 0% -> 3%
where the time goes in v1:
time: 1330 us; the launch traced here: 1320 us
  Pallas kernels  569 us (43%)
  waiting for transfers between devices  244 us (18%)
  blocking collectives  171 us (13%)
  matrix products  113 us (8%)
  local copies, waits for them, and re-layouts  98.5 us (7%)
  other arithmetic  90.4 us (7%)
  between operations  26.1 us (2%)
    pallas_call x6, Pallas kernels, rows_over_mp(): pl.pallas_call(body, name=name, out_shape=out_shape, in_specs=[VMEM_SPEC]...  173 us
    psum x1, waiting for transfers between devices, per_device(): lax.psum((total * jnp.exp(high - row_high), hit), ('dp', 'mp'))  120 us
    pallas_call x1, Pallas kernels, scatter_rows(): pl.pallas_call(body, name=name, out_shape=[jax.ShapeDtypeStruct((rows, wi...  106 us
    pallas_call x1, Pallas kernels, gather_rows(): pl.pallas_call(body, name=name, out_shape=jax.ShapeDtypeStruct((members,...  103 us
    unnamed x7, waiting for transfers between devices  81.2 us
    pallas_call x1, Pallas kernels, head_backward(): pl.pallas_call(body, name='head_backward', grid=(tokens // tile,), out_sh...  77.8 us
    pallas_call x1, Pallas kernels, head_forward(): pl.pallas_call(body, name='head_forward', grid=(tokens // tile,), out_sha...  61.7 us
    unnamed x142, local copies, waits for them, and re-layouts  52 us
  transfers between devices with their start and end apart: 5, of which 4 were waited for; matrix products, arithmetic and copies ran while one was open for 6% of the time, Pallas kernels for 3%

profile of v1, /device:TPU:12, one launch (start us, length us, event | category | flops | bytes accessed | tf_op | source)
XLA Modules:
  0.0 1320.6 jit_solution(1172089923806500090)
XLA Ops:
  15.1 28.0 %all-gather.1 = s32[8,4,1024]{2,1,0:T(4,128)S(1)} all-gather(s32[1,4,1024]{2,1,0:T(4,128)S(1)} %add_bitcast_fusion), channel_id=2, replica_groups=mesh['dp'=8,'mp'=4] {'dp'}, dimensions={0}, use_global_device_ids=true | all-gather | bytes 147456 | tf_op jit(solution)/shard_map/all_gather | solution.py:779
  56.9 66.8 %conditional.4 = (f32[1024,1]{0,1:T(1,128)S(1)}, f32[1024,1024]{1,0:T(8,128)}) conditional(s32[]{:T(128)} %convert_element_type.143, (s32[8,1,1024]{2,1,0:T(1,128)S(1)}, s32[]{:T(128)}, bf16[1584,1024]{1,0:T(8,128)(2,1)}) %tuple.40, (s32[1024]{0:T(1024)}, s32[8,1024]{1,0:T(8,128)S(1)}, s32[]{:T(128)}, s32[8,1,1024]{2,1,0:T(1,128)}, ...), branch_computations={%region_3.7_spmd, %region_7.10_spmd} | conditional | flops 5964184064 | bytes 143118432
  62.5 22.4 %embed_dp.1 = bf16[8,64,1024]{2,1,0:T(8,128)(2,1)S(1)} custom-call(bf16[8,64,1024]{2,1,0:T(8,128)(2,1)S(1)} %bitcast.309), custom_call_target="tpu_custom_call" | custom-call | tf_op jit(solution)/shard_map/cond/branch_1_fun/embed_dp/pallas_call | solution.py:320
  84.9 26.8 %embed_mp.1 = bf16[2,2,512,1024]{3,2,1,0:T(8,128)(2,1)S(1)} custom-call(bf16[512,1024]{1,0:T(8,128)(2,1)S(1)} %bitcast.305), custom_call_target="tpu_custom_call" | custom-call | tf_op jit(solution)/shard_map/cond/branch_1_fun/embed_mp/pallas_call | solution.py:279
  111.8 6.6 multiply_reduce_fusion
  125.5 19.1 %all_gather.22 = bf16[4,1024]{1,0:T(4,128)(2,1)S(1)} all-gather(bf16[4,128]{1,0:T(4,128)(2,1)S(1)} %convert_element_type.146), channel_id=1, replica_groups=mesh['dp'=8,'mp'=4] {'dp'}, dimensions={1}, use_global_device_ids=true | all-gather | bytes 9216 | tf_op jit(solution)/shard_map/all_gather | solution.py:774
  148.7 35.6 %all-gather.10.cloned.1.call-done = bf16[5,1024,256]{1,2,0:T(8,128)(2,1)} async-done(((bf16[5,128,256]{1,2,0:T(8,128)(2,1)}), bf16[5,1024,256]{1,2,0:T(8,128)(2,1)}) %all-gather.10.cloned.1.call-update) | async-done | bytes 2621456 | tf_op jit(solution)/shard_map/all_gather | solution.py:768
  192.7 22.5 %while.27 = (s32[]{:T(128)}, bf16[2,512,4,64]{1,3,2,0:T(8,128)(2,1)S(1)}, f32[2,4,512]{2,1,0:T(4,128)S(1)}, s32[2]{0:T(128)S(1)}, s32[1024]{0:T(1024)S(1)}, /*in...) while((s32[]{:T(128)}, ...), condition=%wide.region_13.14_spmd, body=%wide.region_10.13_spmd.sunk | while | flops 563608064 | bytes 29178040 | solution.py:72
  219.2 33.5 %after_attention.1 = (f32[256,1024]{1,0:T(8,128)S(1)}, bf16[2,2,256,1024]{3,2,1,0:T(8,128)(2,1)S(1)}) custom-call(bf16[2,2,256,1024]{3,2,1,0:T(8,128)(2,1)} %bitcast.328, f32[256,1024]{1,0:T(8,128)S(1)} %constant_dynamic-slice_fusion.refs_1_.refs_2_, f32[1,1024]{1,0:T(1,128)S(1)} %get-tuple-element.503.refs_2_.refs_3_), custom_call_target="tpu_custom_call" | custom-call | tf_op jit(solution)/shard_map/after_attention/pallas_call | solution.py:279
  254.0 7.0 all-gather.8.cloned.1.call-done
  271.9 16.1 %after_ffn.1 = (f32[256,1024]{1,0:T(8,128)S(1)}, bf16[256,1024]{1,0:T(8,128)(2,1)S(1)}) custom-call(bf16[2,2,256,1024]{3,2,1,0:T(8,128)(2,1)S(1)} %bitcast.306, f32[256,1024]{1,0:T(8,128)S(1)} %get-tuple-element.223.refs_1_, f32[1,1024]{1,0:T(1,128)S(1)} %get-tuple-element.502.refs_2_), custom_call_target="tpu_custom_call" | custom-call | tf_op jit(solution)/shard_map/after_ffn/pallas_call | solution.py:279
  288.8 102.8 %gather_hidden.1 = bf16[8,2,2,256,1024]{4,3,2,1,0:T(8,128)(2,1)} custom-call(bf16[256,1024]{1,0:T(8,128)(2,1)} %copy-done.1), custom_call_target="tpu_custom_call" | custom-call | tf_op jit(solution)/shard_map/gather_hidden/pallas_call | solution.py:429
  391.6 61.7 %head_forward.1 = (bf16[1584,8192]{1,0:T(8,128)(2,1)}, f32[1,8192]{1,0:T(1,128)}, f32[1,8192]{1,0:T(1,128)}, f32[1,8192]{1,0:T(1,128)}) custom-call(bf16[8192,1024]{1,0:T(8,128)(2,1)} %bitcast.321, bf16[1584,1024]{1,0:T(8,128)(2,1)} %pad.4.table_ref, s32[1,8192]{1,0:T(1,128)} %compare_select_fusion.3.place_ref), custom_call_target="tpu_custom_call" | custom-call | tf_op jit(solution)/shard_map/head_forward/pallas_call | solution.py:654
  453.3 40.4 %pmax.7 = f32[1,8192]{1,0:T(1,128)S(1)} all-reduce(f32[1,8192]{1,0:T(1,128)} %get-tuple-element.225), channel_id=1, replica_groups=mesh['dp'=8,'mp'=4] {'dp','mp'}, use_global_device_ids=true, to_apply=%region_14.15 | all-reduce | flops 8192 | bytes 65536 | tf_op jit(solution)/shard_map/pmax | solution.py:865
  495.9 120.0 %all-reduce.7.cloned.1.call-done = (f32[1,8192]{1,0:T(1,128)}, f32[1,8192]{1,0:T(1,128)}) async-done(((f32[1,8192]{1,0:T(1,128)}, f32[1,8192]{1,0:T(1,128)}), (f32[1,8192]{1,0:T(1,128)}, f32[1,8192]{1,0:T(1,128)})) %all-reduce.7.cloned.1.call-update) | async-done | bytes 65552 | tf_op jit(solution)/shard_map/psum | solution.py:866
  618.9 77.8 %head_backward.1 = (bf16[8192,1024]{1,0:T(8,128)(2,1)}, f32[1584,1024]{1,0:T(8,128)}) custom-call(bf16[1584,8192]{1,0:T(8,128)(2,1)} %get-tuple-element.228.raised_ref, f32[1,8192]{1,0:T(1,128)} %exponential_multiply_fusion.scale_ref, f32[1,8192]{1,0:T(1,128)} %bitcast.359, s32[1,8192]{1,0:T(1,128)} %compare_select_fusion.3.place_ref, ...), custom_call_target="tpu_custom_call" | custom-call | tf_op jit(solution)/shard_map/head_backward/pallas_call | solution.py:690
  696.7 106.0 %scatter_hidden.1 = (f32[256,1024]{1,0:T(8,128)}, bf16[8,2,256,1024]{3,2,1,0:T(8,128)(2,1)}) custom-call(bf16[8,2,2,256,1024]{4,3,2,1,0:T(8,128)(2,1)} %bitcast.325), custom_call_target="tpu_custom_call" | custom-call | tf_op jit(solution)/shard_map/scatter_hidden/pallas_call | solution.py:611
  803.9 14.4 %before_head.1 = (f32[256,1024]{1,0:T(8,128)S(1)}, f32[1,1024]{1,0:T(1,128)S(1)}, bf16[2,2,256,1024]{3,2,1,0:T(8,128)(2,1)S(1)}) custom-call(f32[256,1024]{1,0:T(8,128)S(1)} %copy-done, f32[256,1024]{1,0:T(8,128)S(1)} %get-tuple-element.233.refs_1_, f32[1,1024]{1,0:T(1,128)S(1)} %get-tuple-element.502.refs_2_), custom_call_target="tpu_custom_call" | custom-call | tf_op jit(solution)/shard_map/before_head/pallas_call | solution.py:279
  829.5 35.4 %before_ffn.1 = (f32[256,1024]{1,0:T(8,128)S(1)}, f32[1,1024]{1,0:T(1,128)S(1)}, bf16[2,2,256,1024]{3,2,1,0:T(8,128)(2,1)S(1)}) custom-call(bf16[2,2,256,1024]{3,2,1,0:T(8,128)(2,1)} %bitcast.337, f32[256,1024]{1,0:T(8,128)S(1)} %get-tuple-element.223.refs_1_, f32[256,1024]{1,0:T(8,128)S(1)} %get-tuple-element.235.refs_2_, ...), custom_call_target="tpu_custom_call" | custom-call | tf_op jit(solution)/shard_map/before_ffn/pallas_call | solution.py:279
  869.0 73.7 %while.28 = (s32[]{:T(128)}, f32[1024,4,64]{0,2,1:T(8,128)}, f32[1024,4,64]{0,2,1:T(8,128)}, f32[2,512,4,64]{1,0,3,2:T(2,128)}, s32[2]{0:T(128)S(1)}, /*index=5*...) while((s32[]{:T(128)}, f32[1024,4,64]{0,2,1:T(8,128)}, ...), condition=%wide.region_24.25_spmd.clone, body=%wide.region_22.24_spmd.clone.sunk | while | flops 1376647680 | bytes 164698512 | solution.py:101
  886.2 10.4 dynamic_update_slice.19
  922.1 10.4 dynamic_update_slice.19
  963.1 46.3 %before_attention.1 = (f32[1,1024]{1,0:T(1,128)S(1)}, f32[1,1024]{1,0:T(1,128)S(1)}, bf16[2,2,256,1024]{3,2,1,0:T(8,128)(2,1)}) custom-call(bf16[2,2,256,1024]{3,2,1,0:T(8,128)(2,1)S(1)} %bitcast.307, bf16[2,2,256,1024]{3,2,1,0:T(8,128)(2,1)} %bitcast.332, f32[256,1024]{1,0:T(8,128)S(1)} %constant_dynamic-slice_fusion.refs_1_.refs_2_, ...), custom_call_target="tpu_custom_call" | custom-call | tf_op jit(solution)/shard_map/before_attention/pallas_call | solution.py:279
  1022.4 33.2 %conditional.10 = (f32[1572,1024]{1,0:T(8,128)}) conditional(s32[]{:T(128)} %convert_element_type.143, (s32[8,1,1024]{2,1,0:T(1,128)S(1)}, s32[]{:T(128)}, bf16[1024,1024]{1,0:T(8,128)(2,1)S(1)}) %tuple.163, (s32[8,1024]{1,0:T(8,128)S(1)}, s32[]{:T(128)}, s32[8,1,1024]{2,1,0:T(1,128)S(1)}, s32[]{:T(128)}, s32[1024]{0:T(1024)S(1)}, ...), branch_computations={%region_25.27_spmd, %region_27.29_spmd} | conditional | flops 2726176768 | bytes 88473688 | solution.py:980
  1024.7 26.3 %table_dp.1 = bf16[8,64,1024]{2,1,0:T(8,128)(2,1)S(1)} custom-call(bf16[8,64,1024]{2,1,0:T(8,128)(2,1)S(1)} %bitcast.310), custom_call_target="tpu_custom_call" | custom-call | tf_op jit(solution)/shard_map/cond/branch_1_fun/table_dp/pallas_call | solution.py:320
  1066.1 10.1 copy.121
  1076.1 12.7 reshape.621
  1091.1 43.0 %psum.37 = f32[4,1024]{1,0:T(4,128)S(1)} all-reduce(f32[4,1024]{1,0:T(4,128)S(1)} %pad_maximum_fusion.14), channel_id=1, replica_groups=mesh['dp'=8,'mp'=4] {'dp','mp'}, use_global_device_ids=true, to_apply=%region_36.37 | all-reduce | flops 4096 | bytes 32768 | tf_op jit(solution)/shard_map/psum | solution.py:981
  1136.5 7.0 multiply_reduce_fusion.3
  1148.6 79.9 %reduce-scatter.12.cloned.1.call-done = bf16[128,2112]{1,0:T(8,128)(2,1)} async-done(((bf16[1024,2112]{1,0:T(8,128)(2,1)}), bf16[128,2112]{1,0:T(8,128)(2,1)}) %reduce-scatter.12.cloned.1.call-update) | async-done | bytes 540688
  1235.0 40.0 %psum.38 = f32[]{:T(128)} all-reduce(f32[]{:T(128)S(6)} %add.363), channel_id=1, replica_groups=mesh['dp'=8,'mp'=4] {'dp','mp'}, use_global_device_ids=true, to_apply=%region_38.39 | all-reduce | flops 1 | bytes 8 | tf_op jit(solution)/shard_map/psum | solution.py:991
  1290.7 19.6 %multiply_add_fusion = (f32[1572,1024]{1,0:T(8,128)}, f32[1572,1024]{1,0:T(8,128)}, f32[1572,1024]{1,0:T(8,128)}) fusion(f32[1572,1024]{1,0:T(8,128)} %param.48, f32[1572,1024]{1,0:T(8,128)} %param.36, f32[]{:T(128)S(6)} %min.3, f32[1572,1024]{1,0:T(8,128)} %get-tuple-element.734, f32[1584,1024]{1,0:T(8,128)} %get-tuple-element.229, f32[1572,1024]{1,0:T(8,128)} %param.42), kind=kLoop, calls=%fused_computation.113 | loop fusion | flops 17707008 | bytes 51511300 | tf_op jit(solution)/shard_map/add | solution.py:999
  (314 shorter events, 226.5 us)
Async XLA Ops:
  56.8 67.5 %copy-start.21 = (f32[2,128,704]{1,2,0:T(8,128)S(1)}, f32[2,128,704]{1,2,0:T(8,128)}, u32[]{:S(2)}) copy-start(f32[2,128,704]{1,2,0:T(8,128)} %param.39) | copy-start | bytes 2162692
  56.8 67.6 %copy-start.28 = (f32[704,128]{1,0:T(8,128)S(1)}, f32[704,128]{1,0:T(8,128)}, u32[]{:S(2)}) copy-start(f32[704,128]{1,0:T(8,128)} %param.40) | copy-start | bytes 1081348
  56.8 68.6 %copy-start.54 = (f32[4,128]{1,0:T(4,128)S(1)}, f32[4,128]{1,0:T(4,128)}, u32[]{:S(2)}) copy-start(f32[4,128]{1,0:T(4,128)} %param.41) | copy-start | bytes 6148
  56.8 89.0 %copy-start.43 = (s32[8,1,1024]{2,1,0:T(1,128)S(1)}, s32[8,1,1024]{2,1,0:T(1,128)}, u32[]{:S(2)}) copy-start(s32[8,1,1024]{2,1,0:T(1,128)} %get-tuple-element.501) | copy-start | bytes 98308
  56.9 89.2 %copy-start.63 = (s32[8]{0:T(128)S(1)}, s32[8]{0:T(128)}, u32[]{:S(2)}) copy-start(s32[8]{0:T(128)} %param.35) | copy-start | bytes 100
  62.5 49.2 %copy-start.59 = (s32[1024]{0:T(1024)S(1)}, s32[1024]{0:T(1024)}, u32[]{:S(2)}) copy-start(s32[1024]{0:T(1024)} %get-tuple-element.134) | copy-start | bytes 12292 | tf_op jit(solution)/shard_map/conditional.1
  123.7 24.3 %copy-start.49 = (s32[8,1,1024]{2,1,0:T(1,128)S(1)}, s32[8,1,1024]{2,1,0:T(1,128)}, u32[]{:S(2)}) copy-start(s32[8,1,1024]{2,1,0:T(1,128)} %get-tuple-element.497) | copy-start | bytes 98308
  123.7 24.3 %copy-start.50 = (s32[8,1,1024]{2,1,0:T(1,128)S(1)}, s32[8,1,1024]{2,1,0:T(1,128)}, u32[]{:S(2)}) copy-start(s32[8,1,1024]{2,1,0:T(1,128)} %get-tuple-element.498) | copy-start | bytes 98308
  123.7 24.3 %copy-start.51 = (pred[8,1,1024]{2,1,0:T(4,128)(4,1)S(1)}, pred[8,1,1024]{2,1,0:T(4,128)(4,1)}, u32[]{:S(2)}) copy-start(pred[8,1,1024]{2,1,0:T(4,128)(4,1)} %get-tuple-element.495) | copy-start | bytes 24580
  123.7 60.6 %all-gather.10.cloned.1.call-start = ((), (), s32[]{:S(2)}) async-start(), calls=%async_computation.7 | async-start | bytes 2949120 | tf_op jit(solution)/shard_map/all_gather | solution.py:768
  124.3 136.7 %all-gather.8.cloned.1.call-start = ((), (), s32[]{:S(2)}) async-start(), calls=%async_computation.6 | async-start | bytes 4866048 | tf_op jit(solution)/shard_map/all_gather | solution.py:771
  125.3 490.6 %all-reduce.7.cloned.1.call-start = ((), (), s32[]{:S(2)}) async-start(), calls=%async_computation.10 | async-start | bytes 131072 | tf_op jit(solution)/shard_map/psum | solution.py:866
  125.4 64.1 %copy-start.52 = (f32[1024,1]{0,1:T(1,128)}, f32[1024,1]{0,1:T(1,128)S(1)}, u32[]{:S(2)}) copy-start(f32[1024,1]{0,1:T(1,128)S(1)} %add_rsqrt_fusion) | copy-start | bytes 12292
  144.6 44.3 %copy-start.4 = (f32[1,1024]{1,0:T(1,128)}, f32[1,1024]{1,0:T(1,128)S(1)}, u32[]{:S(2)}) copy-start(f32[1,1024]{1,0:T(1,128)S(1)} %get-tuple-element.505.refs_5_) | copy-start | bytes 12292
  144.6 44.9 %copy-start.2 = (f32[1,1024]{1,0:T(1,128)}, f32[1,1024]{1,0:T(1,128)S(1)}, u32[]{:S(2)}) copy-start(f32[1,1024]{1,0:T(1,128)S(1)} %get-tuple-element.504.refs_4_) | copy-start | bytes 12292
  145.8 43.2 %copy-start.31 = (f32[1024,32]{0,1:T(8,128)}, f32[1024,32]{0,1:T(8,128)S(1)}, u32[]{:S(2)}) copy-start(f32[1024,32]{0,1:T(8,128)S(1)} %get-tuple-element.508) | copy-start | bytes 393220
  146.0 349.2 %copy-start.56 = (f32[8]{0:T(128)}, f32[8]{0:T(128)S(1)}, u32[]{:S(2)}) copy-start(f32[8]{0:T(128)S(1)} %convert_reduce_fusion.1) | copy-start | bytes 100
  215.2 37.5 %copy-start.12 = (bf16[1024,4,64]{0,2,1:T(8,128)(2,1)}, bf16[1024,4,64]{0,2,1:T(8,128)(2,1)S(1)}, u32[]{:S(2)}) copy-start(bf16[1024,4,64]{0,2,1:T(8,128)(2,1)S(1)} %get-tuple-element.744) | copy-start | bytes 1572868
  215.2 37.4 %copy-start.14 = (bf16[1024,4,64]{0,2,1:T(8,128)(2,1)}, bf16[1024,4,64]{0,2,1:T(8,128)(2,1)S(1)}, u32[]{:S(2)}) copy-start(bf16[1024,4,64]{0,2,1:T(8,128)(2,1)S(1)} %get-tuple-element.747) | copy-start | bytes 1572868
  803.9 20.8 %slice-start = ((s8[4325376]{0:T(1024)(128)(4,1)}), s8[131072]{0:T(1024)(128)(4,1)S(1)}, s32[]{:S(2)}) async-start(s8[4325376]{0:T(1024)(128)(4,1)} %bitcast.384), calls=%async_computation.11 | async-start | bytes 262144
  829.5 35.4 %copy-start.26 = (bf16[32,8,2,512]{3,1,2,0:T(8,128)(2,1)S(1)}, bf16[32,8,2,512]{3,1,2,0:T(8,128)(2,1)}, u32[]{:S(2)}) copy-start(bf16[32,8,2,512]{3,1,2,0:T(8,128)(2,1)} %copy-done.25) | copy-start | bytes 1572868
  869.0 75.8 %copy-start.32 = (f32[1024,32]{0,1:T(8,128)S(1)}, f32[1024,32]{0,1:T(8,128)}, u32[]{:S(2)}) copy-start(f32[1024,32]{0,1:T(8,128)} %copy-done.31) | copy-start | bytes 393220
  961.0 48.4 %copy-start.37 = (bf16[1,1024,256]{1,2,0:T(8,128)(2,1)S(1)}, bf16[1,1024,256]{1,2,0:T(8,128)(2,1)}, u32[]{:S(2)}) copy-start(bf16[1,1024,256]{1,2,0:T(8,128)(2,1)} %fusion.92) | copy-start | bytes 1572868
  1055.6 87.9 %reduce-scatter.10.cloned.1.call-start = ((), (), s32[]{:S(2)}) async-start(), calls=%async_computation.8 | async-start | bytes 2949120
  1056.3 172.1 %reduce-scatter.12.cloned.1.call-start = ((), (), s32[]{:S(2)}) async-start(), calls=%async_computation.9 | async-start | bytes 5013504
  1088.8 46.5 %copy-start.57 = (f32[8]{0:T(128)S(1)}, f32[8]{0:T(128)}, u32[]{:S(2)}) copy-start(f32[8]{0:T(128)} %copy-done.56) | copy-start | bytes 100
  1088.8 46.5 %copy-start.60 = (f32[8]{0:T(128)S(1)}, f32[8]{0:T(128)}, u32[]{:S(2)}) copy-start(f32[8]{0:T(128)} %get-tuple-element.399) | copy-start | bytes 100
  1088.8 46.5 %copy-start.64 = (s32[8]{0:T(128)S(1)}, s32[8]{0:T(128)}, u32[]{:S(2)}) copy-start(s32[8]{0:T(128)} %param.35) | copy-start | bytes 100
  1143.5 132.2 %copy-start.18 = (f32[4,128,256]{1,2,0:T(8,128)S(1)}, f32[4,128,256]{1,2,0:T(8,128)}, u32[]{:S(2)}) copy-start(f32[4,128,256]{1,2,0:T(8,128)} %copy.96) | copy-start | bytes 1572868
  1230.8 53.4 %copy-start.55 = (f32[4,128]{1,0:T(4,128)S(1)}, f32[4,128]{1,0:T(4,128)}, u32[]{:S(2)}) copy-start(f32[4,128]{1,0:T(4,128)} %param.41) | copy-start | bytes 6148
  1230.8 53.4 %copy-start.61 = (f32[4,128]{1,0:T(4,128)S(1)}, f32[4,128]{1,0:T(4,128)}, u32[]{:S(2)}) copy-start(f32[4,128]{1,0:T(4,128)} %param.53) | copy-start | bytes 6148
  1230.8 53.4 %copy-start.62 = (f32[4,128]{1,0:T(4,128)S(1)}, f32[4,128]{1,0:T(4,128)}, u32[]{:S(2)}) copy-start(f32[4,128]{1,0:T(4,128)} %param.47) | copy-start | bytes 6148
  (49 other events, 226.4 us)
Sparse Core Ops, SparseCore 1:
  126.8 57.5 all-gather.9
  186.8 74.1 all-gather.7
  495.3 120.5 all-reduce.6
  1059.9 72.5 reduce-scatter.9
  1136.7 91.7 reduce-scatter.11
